TPU v7x, 32 devices: a 4x4x1 block of a 4x4x8 slice. The times are simulated.
32 devices in a mesh: rep: 2 (over z, core), dp: 16 (over x, y).
Axes of the slice: x: 4, y: 4, z: 1, core: 2. Of those that a mesh axis runs over, the one named last changes fastest.
The devices are a block of a 4x4x8 slice.
Arguments:
- x: bfloat16 [32, 2048, 1024], P(('rep', 'dp')), parts along dimension 0
- dy: bfloat16 [32, 2048, 1024], P(('rep', 'dp')), parts along dimension 0
- w_gate: bfloat16 [2, 1024, 3200], replicated
- w_up: bfloat16 [2, 1024, 3200], replicated
- w_down: bfloat16 [2, 3200, 1024], replicated
- m_w_gate: float32 [2, 1024, 3200], P(None, 'dp')
- m_w_up: float32 [2, 1024, 3200], P(None, 'dp')
- m_w_down: float32 [2, 3200, 1024], P(None, 'dp')
- v_w_gate: float32 [2, 1024, 3200], P(None, 'dp')
- v_w_up: float32 [2, 1024, 3200], P(None, 'dp')
- v_w_down: float32 [2, 3200, 1024], P(None, 'dp')
Outputs:
- output 1: bfloat16 [4, 1024, 3200], P('rep'), parts along dimension 0
- output 2: bfloat16 [4, 1024, 3200], P('rep'), parts along dimension 0
- output 3: bfloat16 [4, 3200, 1024], P('rep'), parts along dimension 0
- output 4: float32 [4, 1024, 3200], P('rep', 'dp'), parts along dimension 0
- output 5: float32 [4, 1024, 3200], P('rep', 'dp'), parts along dimension 0
- output 6: float32 [4, 3200, 1024], P('rep', 'dp'), parts along dimension 0
- output 7: float32 [4, 1024, 3200], P('rep', 'dp'), parts along dimension 0
- output 8: float32 [4, 1024, 3200], P('rep', 'dp'), parts along dimension 0
- output 9: float32 [4, 3200, 1024], P('rep', 'dp'), parts along dimension 0
There are 2 independent parts. A program takes and returns all parts, laid end to end along the dimension named above; an argument that names none is the same for every part.
All inputs are finite; a program needn't handle non-finite values.
Results may differ from a plain program's by a relative error of at most 0.022.
Values are sent between devices in bfloat16 or wider.
A program may use at most 768 MiB of HBM per device.

v0:
```python
import jax
import jax.numpy as jnp
from jax import lax

NAMES = ("w_gate", "w_up", "w_down")


def matmul(a, w):
    return jnp.dot(a, w, preferred_element_type=jnp.float32).astype(jnp.bfloat16)


def normed(h):
    wide = h.astype(jnp.float32)
    scale = lax.rsqrt(jnp.mean(wide**2, -1, keepdims=True) + 1e-6)
    return (wide * scale).astype(jnp.bfloat16)


def layer(h, w):
    a = normed(h)
    gate = jnp.dot(a, w["w_gate"], preferred_element_type=jnp.float32)
    up = jnp.dot(a, w["w_up"], preferred_element_type=jnp.float32)
    return h + matmul((jax.nn.silu(gate) * up).astype(jnp.bfloat16), w["w_down"])


def adamw(w, m, v, g):
    m = 0.9 * m + 0.1 * g
    v = 0.95 * v + 0.05 * g * g
    step = m * lax.rsqrt(v + 1e-8) + 0.1 * w
    return (w - 0.02 * step).astype(jnp.bfloat16), m, v


def stack(weights, h):
    for number in range(weights["w_gate"].shape[0]):
        h = layer(h, {name: w[number] for name, w in weights.items()})
    return h


def solution(mesh):
    groups = mesh.shape["rep"]

    def step(x, dy, *arrays):
        weights, m, v = (arrays[i : i + 3] for i in (0, 3, 6))
        x, dy = (t.reshape(groups, -1, *t.shape[1:]) for t in (x, dy))

        def of_a_group(x, dy):
            _, back = jax.vjp(lambda w: stack(w, x), dict(zip(NAMES, weights, strict=True)))
            by_weights = back(dy)[0]
            gradients = [by_weights[name].astype(jnp.float32) for name in NAMES]
            new = [adamw(w.astype(jnp.float32), m, v, g) for w, m, v, g in zip(weights, m, v, gradients, strict=True)]
            return tuple(one[which] for which in range(3) for one in new)

        return tuple(t.reshape(-1, *t.shape[2:]) for t in jax.vmap(of_a_group)(x, dy))

    return step
```

profile of v0, /device:TPU:96, one launch (start us, length us, event | category | flops | bytes accessed | tf_op | source)
XLA Modules:
  0.0 1067.3 jit_solution(2867342246792766561)
XLA Ops:
  7.3 3.1 fusion.47
  10.3 6.6 copy
  17.0 22.0 %fusion.67 = f32[2048,3200]{1,0:T(8,128)} fusion(bf16[2,1024,3200]{2,1,0:T(8,128)(2,1)} %param, bf16[1,2048,1024]{2,1,0:T(8,128)(2,1)} %param.2, f32[2048]{0:T(1024)S(1)} %add_rsqrt_fusion), kind=kOutput, calls=%fused_computation.79 | convolution fusion | flops 13428064256 | bytes 36970496 | tf_op jit(solution)/vmap(jvp())/dot_general | solution.py:20
  39.0 18.1 %fusion.65 = f32[2048,3200]{1,0:T(8,128)} fusion(bf16[2,1024,3200]{2,1,0:T(8,128)(2,1)S(1)} %bitcast.342, bf16[1,2048,1024]{2,1,0:T(8,128)(2,1)S(1)} %copy-done.1, f32[2048]{0:T(1024)S(1)} %add_rsqrt_fusion), kind=kOutput, calls=%fused_computation.77 | convolution fusion | flops 13428064256 | bytes 36970496 | tf_op jit(solution)/vmap(jvp())/dot_general | solution.py:21
  57.1 22.9 %fusion.26 = bf16[2048,3200]{1,0:T(8,128)(2,1)} fusion(f32[2048,3200]{1,0:T(8,128)} %fusion.65, f32[2048,3200]{1,0:T(8,128)} %fusion.67), kind=kLoop, calls=%fused_computation.41 | loop fusion | flops 39321600 | bytes 65536000
  80.0 22.3 %fusion.51 = (f32[2048]{0:T(1024)S(1)}, bf16[1,1,2048,1024]{2,3,1,0:T(8,128)(2,1)}) fusion(bf16[2048,3200]{1,0:T(8,128)(2,1)} %fusion.26, bf16[2,3200,1024]{2,1,0:T(8,128)(2,1)} %param.4, bf16[1,2048,1024]{1,2,0:T(8,128)(2,1)} %copy), kind=kOutput, calls=%fused_computation.62 | convolution fusion | flops 13432256512 | bytes 28057600 | tf_op jit(solution)/vmap(jvp())/dot_general | solution.py:9
  102.4 0.6 copy-done.10
  103.0 23.1 %fusion.54 = f32[2048,3200]{1,0:T(8,128)} fusion(bf16[2,1024,3200]{2,1,0:T(8,128)(2,1)} %param, bf16[1,1,2048,1024]{2,3,1,0:T(8,128)(2,1)} %get-tuple-element.10, f32[2048]{0:T(1024)S(1)} %bitcast.344), kind=kOutput, calls=%fused_computation.66 | convolution fusion | flops 13428064256 | bytes 36970496 | tf_op jit(solution)/vmap(jvp())/dot_general | solution.py:20
  126.1 20.8 %fusion.58 = f32[2048,3200]{1,0:T(8,128)} fusion(bf16[2,1024,3200]{2,1,0:T(8,128)(2,1)} %param.3, bf16[1,1,2048,1024]{2,3,1,0:T(8,128)(2,1)S(1)} %copy-done.3, f32[2048]{0:T(1024)S(1)} %bitcast.345), kind=kOutput, calls=%fused_computation.70 | convolution fusion | flops 13428064256 | bytes 36970496 | tf_op jit(solution)/vmap(jvp())/dot_general | solution.py:21
  146.9 28.7 %fusion.35 = f32[1,3200,1024]{2,1,0:T(8,128)} fusion(f32[2048,3200]{1,0:T(8,128)} %fusion.58, f32[2048,3200]{1,0:T(8,128)} %fusion.54, bf16[1,2048,1024]{2,1,0:T(8,128)(2,1)} %param.5), kind=kOutput, calls=%fused_computation.52 | convolution fusion | flops 13461094400 | bytes 69730304 | tf_op jit(solution)/vmap(transpose(jvp()))/dot_general | solution.py:9
  175.8 6.5 copy.1
  182.3 20.8 %convolution_convert_fusion.1 = bf16[2048,3200]{1,0:T(8,128)(2,1)} fusion(bf16[2,3200,1024]{2,1,0:T(8,128)(2,1)} %param.4, bf16[1,2048,1024]{2,1,0:T(8,128)(2,1)} %param.5), kind=kOutput, calls=%fused_computation.36 | convolution fusion | flops 13428326400 | bytes 23855104 | tf_op jit(solution)/vmap(transpose(jvp()))/dot_general | solution.py:9
  203.1 26.9 %fusion.6 = bf16[2048,3200]{1,0:T(8,128)(2,1)} fusion(f32[2048,3200]{1,0:T(8,128)} %fusion.54, f32[2048,3200]{1,0:T(8,128)} %fusion.58, bf16[2048,3200]{1,0:T(8,128)(2,1)} %convolution_convert_fusion.1), kind=kLoop, calls=%fused_computation.11 | loop fusion | flops 78643200 | bytes 78643200
  229.9 22.6 %fusion.24 = bf16[2048,1024]{0,1:T(8,128)(2,1)} fusion(bf16[2048,3200]{1,0:T(8,128)(2,1)} %convolution_convert_fusion.1, f32[2048,3200]{1,0:T(8,128)} %fusion.54, bf16[2,1024,3200]{2,1,0:T(8,128)(2,1)} %param.3), kind=kOutput, calls=%fused_computation.34 | convolution fusion | flops 13461094400 | bytes 50069504 | tf_op jit(solution)/vmap(transpose(jvp()))/dot_general | solution.py:21
  252.5 23.0 %fusion.53 = (f32[2048]{0:T(1024)S(1)}, bf16[2048,1024]{0,1:T(8,128)(2,1)}) fusion(bf16[1,1,2048,1024]{2,3,1,0:T(8,128)(2,1)} %get-tuple-element.10, bf16[2048,1024]{0,1:T(8,128)(2,1)} %fusion.24, bf16[2048,3200]{1,0:T(8,128)(2,1)} %fusion.6, bf16[2,1024,3200]{2,1,0:T(8,128)(2,1)} %param), kind=kOutput, calls=%fused_computation.64 | convolution fusion | flops 13432256512 | bytes 32251904 | tf_op jit(solution)/vmap(transpose(jvp()))/dot_general | solution.py:20
  275.6 5.3 fusion.81
  281.0 2.0 copy-done.4
  282.9 19.8 %convolution_bitcast_fusion.1 = f32[1,3200,1024]{2,1,0:T(8,128)} fusion(bf16[2048,3200]{1,0:T(8,128)(2,1)} %fusion.26, bf16[2048,1024]{0,1:T(8,128)(2,1)S(1)} %fusion.81), kind=kOutput, calls=%fused_computation.57 | convolution fusion | flops 13421772800 | bytes 30408704 | tf_op jit(solution)/vmap(transpose(jvp()))/dot_general | solution.py:9
  302.8 22.0 %convolution_bitcast_fusion = f32[1,1024,3200]{2,1,0:T(8,128)} fusion(bf16[2048,3200]{1,0:T(8,128)(2,1)} %fusion.6, bf16[1,1,2048,1024]{2,3,1,0:T(8,128)(2,1)} %get-tuple-element.10, f32[2048]{0:T(1024)S(1)} %bitcast.347), kind=kOutput, calls=%fused_computation.55 | convolution fusion | flops 13428064256 | bytes 30416896 | tf_op jit(solution)/vmap(transpose(jvp()))/dot_general | solution.py:20
  325.0 21.5 %convolution_convert_fusion = bf16[2048,3200]{1,0:T(8,128)(2,1)} fusion(bf16[2048,1024]{0,1:T(8,128)(2,1)} %copy-done.4, bf16[2,3200,1024]{2,1,0:T(8,128)(2,1)} %param.4), kind=kOutput, calls=%fused_computation.35 | convolution fusion | flops 13428326400 | bytes 23855104 | tf_op jit(solution)/vmap(transpose(jvp()))/dot_general | solution.py:9
  346.5 31.9 %fusion.44 = f32[1,1024,3200]{2,1,0:T(8,128)} fusion(f32[2048,3200]{1,0:T(8,128)} %fusion.67, f32[2048,3200]{1,0:T(8,128)} %fusion.65, bf16[2048,3200]{1,0:T(8,128)(2,1)} %convolution_convert_fusion, bf16[1,2048,1024]{1,2,0:T(8,128)(2,1)S(1)} %copy-done.5, f32[2048]{0:T(1024)S(1)} %copy-done.15), kind=kOutput, calls=%fused_computation.56 | convolution fusion | flops 13500153856 | bytes 82845696 | tf_op jit(solution)/vmap(transpose(jvp()))/dot_general | solution.py:20
  378.6 26.0 %fusion.38 = f32[1,1024,3200]{2,1,0:T(8,128)} fusion(bf16[2048,3200]{1,0:T(8,128)(2,1)} %convolution_convert_fusion.1, f32[2048,3200]{1,0:T(8,128)} %fusion.54, bf16[1,1,2048,1024]{2,3,1,0:T(8,128)(2,1)} %get-tuple-element.10, f32[2048]{0:T(1024)S(1)} %bitcast.348), kind=kOutput, calls=%fused_computation.53 | convolution fusion | flops 13467385856 | bytes 56631296 | tf_op jit(solution)/vmap(transpose(jvp()))/dot_general | solution.py:21
  404.7 25.8 %fusion.41 = f32[1,1024,3200]{2,1,0:T(8,128)} fusion(bf16[2048,3200]{1,0:T(8,128)(2,1)} %convolution_convert_fusion, f32[2048,3200]{1,0:T(8,128)} %fusion.67, bf16[1,2048,1024]{1,2,0:T(8,128)(2,1)} %copy, f32[2048]{0:T(1024)S(1)} %copy-done.15), kind=kOutput, calls=%fused_computation.54 | convolution fusion | flops 13467385856 | bytes 56631296 | tf_op jit(solution)/vmap(transpose(jvp()))/dot_general | solution.py:21
  430.6 0.3 all-gather.14.cloned.1.call-start
  430.9 0.3 copy-done.16
  431.2 0.6 dynamic-slice
  432.4 2.0 convert_bitcast_fusion.4
  434.4 1.2 convert_bitcast_fusion.3
  435.6 4.2 fusion.121
  439.9 0.1 all-gather.10.cloned.1.call-start
  440.0 48.8 %reduce-scatter.23.cloned.1.call-done = f32[1,64,3200]{2,1,0:T(8,128)} async-done(((f32[1,1024,3200]{2,1,0:T(8,128)}), f32[1,64,3200]{2,1,0:T(8,128)}) %reduce-scatter.23.cloned.1.call-update) | async-done | bytes 819216
  488.8 1.9 convert_bitcast_fusion.8
  490.7 91.2 %reduce-scatter.25.cloned.1.call-done = f32[1,64,3200]{2,1,0:T(8,128)} async-done(((f32[1,1024,3200]{2,1,0:T(8,128)}), f32[1,64,3200]{2,1,0:T(8,128)}) %reduce-scatter.25.cloned.1.call-update) | async-done | bytes 819216
  581.9 1.2 convert_bitcast_fusion.7
  583.1 5.1 fusion.123
  588.4 86.1 %reduce-scatter.27.cloned.1.call-done = f32[1,64,3200]{2,1,0:T(8,128)} async-done(((f32[1,1024,3200]{2,1,0:T(8,128)}), f32[1,64,3200]{2,1,0:T(8,128)}) %reduce-scatter.27.cloned.1.call-update) | async-done | bytes 819216
  674.5 1.9 convert_bitcast_fusion.6
  676.4 91.1 %reduce-scatter.29.cloned.1.call-done = f32[1,64,3200]{2,1,0:T(8,128)} async-done(((f32[1,1024,3200]{2,1,0:T(8,128)}), f32[1,64,3200]{2,1,0:T(8,128)}) %reduce-scatter.29.cloned.1.call-update) | async-done | bytes 819216
  767.5 1.2 convert_bitcast_fusion.5
  768.7 4.1 fusion.122
  772.9 82.4 %all-gather.14.cloned.1.call-done = bf16[1,2,3200,1024]{3,2,1,0:T(8,128)(2,1)} async-done(((bf16[1,2,200,1024]{3,2,1,0:T(8,128)(2,1)}), bf16[1,2,3200,1024]{3,2,1,0:T(8,128)(2,1)}) %all-gather.14.cloned.1.call-update) | async-done | bytes 13107216 | tf_op jit(solution)/reshape | solution.py:52
  855.2 89.3 %all-gather.10.cloned.1.call-done = bf16[1,2,1024,3200]{3,2,1,0:T(8,128)(2,1)} async-done(((bf16[1,2,64,3200]{3,2,1,0:T(8,128)(2,1)}), bf16[1,2,1024,3200]{3,2,1,0:T(8,128)(2,1)}) %all-gather.10.cloned.1.call-update) | async-done | bytes 13107216 | tf_op jit(solution)/reshape | solution.py:52
  944.5 89.3 %all-gather.12.cloned.1.call-done = bf16[1,2,1024,3200]{3,2,1,0:T(8,128)(2,1)} async-done(((bf16[1,2,64,3200]{3,2,1,0:T(8,128)(2,1)}), bf16[1,2,1024,3200]{3,2,1,0:T(8,128)(2,1)}) %all-gather.12.cloned.1.call-update) | async-done | bytes 13107216 | tf_op jit(solution)/reshape | solution.py:52
  1033.8 12.7 %copy.9 = bf16[2,1024,3200]{2,1,0:T(8,128)(2,1)} copy(bf16[2,1024,3200]{2,1,0:T(8,128)(2,1)} %bitcast.337) | data formatting | bytes 26214400
  1046.5 6.6 copy.10
  1053.1 1.2 slice-done.1
  1054.3 1.3 slice-done.2
  1055.6 4.9 copy.11
  (69 shorter events, 1.2 us)
Async XLA Ops:
  7.2 425.2 %reduce-scatter.31.cloned.1.call-start = ((), (), s32[]{:S(2)}) async-start(), calls=%async_computation.13 | async-start | bytes 13926400
  10.3 28.6 %slice-start.4 = ((s8[13107200]{0:T(1024)(128)(4,1)}), s8[524288]{0:T(1024)(128)(4,1)S(1)}, s32[]{:S(2)}) async-start(s8[13107200]{0:T(1024)(128)(4,1)} %bitcast.341), calls=%async_computation.19 | async-start | bytes 1048576
  16.9 22.1 %copy-start.14 = (f32[2048]{0:T(1024)}, f32[2048]{0:T(1024)S(1)}, u32[]{:S(2)}) copy-start(f32[2048]{0:T(1024)S(1)} %add_rsqrt_fusion) | copy-start | bytes 24580
  16.9 22.1 %copy-start.1 = (bf16[1,2048,1024]{2,1,0:T(8,128)(2,1)S(1)}, bf16[1,2048,1024]{2,1,0:T(8,128)(2,1)}, u32[]{:S(2)}) copy-start(bf16[1,2048,1024]{2,1,0:T(8,128)(2,1)} %param.2) | copy-start | bytes 12582916
  16.9 22.1 %slice-start.5 = ((s8[13107200]{0:T(1024)(128)(4,1)}), s8[4194304]{0:T(1024)(128)(4,1)S(1)}, s32[]{:S(2)}) async-start(s8[13107200]{0:T(1024)(128)(4,1)} %bitcast.341), calls=%async_computation.20 | async-start | bytes 8388608
  16.9 22.1 %slice-start.6 = ((s8[13107200]{0:T(1024)(128)(4,1)}), s8[4194304]{0:T(1024)(128)(4,1)S(1)}, s32[]{:S(2)}) async-start(s8[13107200]{0:T(1024)(128)(4,1)} %bitcast.341), calls=%async_computation.21 | async-start | bytes 8388608
  16.9 22.1 %slice-start.7 = ((s8[13107200]{0:T(1024)(128)(4,1)}), s8[4194304]{0:T(1024)(128)(4,1)S(1)}, s32[]{:S(2)}) async-start(s8[13107200]{0:T(1024)(128)(4,1)} %bitcast.341), calls=%async_computation.22 | async-start | bytes 8388608
  102.4 0.6 copy-start.10
  102.4 23.7 %copy-start.12 = (f32[1,1,2048]{2,1,0:T(1,128)}, f32[1,1,2048]{2,1,0:T(1,128)S(1)}, u32[]{:S(2)}) copy-start(f32[1,1,2048]{2,1,0:T(1,128)S(1)} %rsqrt.31) | copy-start | bytes 24580
  103.0 23.1 %copy-start.3 = (bf16[1,1,2048,1024]{2,3,1,0:T(8,128)(2,1)S(1)}, bf16[1,1,2048,1024]{2,3,1,0:T(8,128)(2,1)}, u32[]{:S(2)}) copy-start(bf16[1,1,2048,1024]{2,3,1,0:T(8,128)(2,1)} %get-tuple-element.10) | copy-start | bytes 12582916
  175.7 258.7 %reduce-scatter.33.cloned.1.call-start = ((), (), s32[]{:S(2)}) async-start(), calls=%async_computation.14 | async-start | bytes 13926400
  252.5 23.0 %copy-start.11 = (f32[2048]{0:T(1024)S(1)}, f32[2048]{0:T(1024)}, u32[]{:S(2)}) copy-start(f32[2048]{0:T(1024)} %copy-done.10) | copy-start | bytes 24580
  252.5 23.1 %copy-start = (bf16[1,2048,1024]{1,2,0:T(8,128)(2,1)S(1)}, bf16[1,2048,1024]{1,2,0:T(8,128)(2,1)}, u32[]{:S(2)}) copy-start(bf16[1,2048,1024]{1,2,0:T(8,128)(2,1)} %copy.1) | copy-start | bytes 12582916
  252.5 23.1 %copy-start.13 = (f32[1,1,2048]{2,1,0:T(1,128)S(1)}, f32[1,1,2048]{2,1,0:T(1,128)}, u32[]{:S(2)}) copy-start(f32[1,1,2048]{2,1,0:T(1,128)} %copy-done.12) | copy-start | bytes 24580
  280.9 2.0 copy-start.4
  302.7 186.0 %reduce-scatter.23.cloned.1.call-start = ((), (), s32[]{:S(2)}) async-start(), calls=%async_computation.9 | async-start | bytes 13926400
  324.9 21.6 %copy-start.15 = (f32[2048]{0:T(1024)S(1)}, f32[2048]{0:T(1024)}, u32[]{:S(2)}) copy-start(f32[2048]{0:T(1024)} %copy-done.14) | copy-start | bytes 24580
  324.9 257.0 %reduce-scatter.25.cloned.1.call-start = ((), (), s32[]{:S(2)}) async-start(), calls=%async_computation.10 | async-start | bytes 13926400
  325.0 21.5 %copy-start.5 = (bf16[1,2048,1024]{1,2,0:T(8,128)(2,1)S(1)}, bf16[1,2048,1024]{1,2,0:T(8,128)(2,1)}, u32[]{:S(2)}) copy-start(bf16[1,2048,1024]{1,2,0:T(8,128)(2,1)} %copy) | copy-start | bytes 12582916
  378.5 296.0 %reduce-scatter.27.cloned.1.call-start = ((), (), s32[]{:S(2)}) async-start(), calls=%async_computation.11 | async-start | bytes 13926400
  404.6 362.9 %reduce-scatter.29.cloned.1.call-start = ((), (), s32[]{:S(2)}) async-start(), calls=%async_computation.12 | async-start | bytes 13926400
  430.5 0.7 copy-start.16
  430.5 5.1 copy-start.6
  430.5 5.1 copy-start.7
  430.6 424.7 %all-gather.14.cloned.1.call-start = ((), (), s32[]{:S(2)}) async-start(), calls=%async_computation.8 | async-start | bytes 13926400 | tf_op jit(solution)/reshape | solution.py:52
  439.8 328.9 %copy-start.8 = (f32[2,64,3200]{2,1,0:T(8,128)S(1)}, f32[2,64,3200]{2,1,0:T(8,128)}, u32[]{:S(2)}) copy-start(f32[2,64,3200]{2,1,0:T(8,128)} %param.8) | copy-start | bytes 4915204
  439.8 328.9 %copy-start.9 = (f32[2,64,3200]{2,1,0:T(8,128)S(1)}, f32[2,64,3200]{2,1,0:T(8,128)}, u32[]{:S(2)}) copy-start(f32[2,64,3200]{2,1,0:T(8,128)} %param.7) | copy-start | bytes 4915204
  439.9 504.6 %all-gather.10.cloned.1.call-start = ((), (), s32[]{:S(2)}) async-start(), calls=%async_computation.6 | async-start | bytes 13926400 | tf_op jit(solution)/reshape | solution.py:52
  588.3 445.5 %all-gather.12.cloned.1.call-start = ((), (), s32[]{:S(2)}) async-start(), calls=%async_computation.7 | async-start | bytes 13926400 | tf_op jit(solution)/reshape | solution.py:52
  1033.8 12.7 %copy-start.2 = (bf16[1,2,1024,3200]{3,2,1,0:T(8,128)(2,1)S(1)}, bf16[1,2,1024,3200]{3,2,1,0:T(8,128)(2,1)}, u32[]{:S(2)}) copy-start(bf16[1,2,1024,3200]{3,2,1,0:T(8,128)(2,1)} %all-gather.12.cloned.1.call-done) | copy-start | bytes 39321604
  1033.8 19.4 %slice-start = ((s8[13107200]{0:T(1024)(128)(4,1)}), s8[4194304]{0:T(1024)(128)(4,1)S(1)}, s32[]{:S(2)}) async-start(s8[13107200]{0:T(1024)(128)(4,1)} %bitcast.334), calls=%async_computation.15 | async-start | bytes 8388608
  1033.8 20.5 %slice-start.1 = ((s8[13107200]{0:T(1024)(128)(4,1)}), s8[4194304]{0:T(1024)(128)(4,1)S(1)}, s32[]{:S(2)}) async-start(s8[13107200]{0:T(1024)(128)(4,1)} %bitcast.334), calls=%async_computation.16 | async-start | bytes 8388608
  1046.5 9.1 slice-start.2
  1046.5 9.1 slice-start.3
Sparse Core Ops, SparseCore 0:
  175.8 93.1 reduce-scatter.30
  302.9 93.2 reduce-scatter.32
  399.4 89.3 reduce-scatter.22
  492.5 89.3 reduce-scatter.24
  585.0 89.3 reduce-scatter.26
  678.2 89.2 reduce-scatter.28
  769.4 85.7 all-gather.13
  857.8 86.6 all-gather.9
  947.0 86.6 all-gather.11
where the time goes:
time: 1080 us; the launch traced here: 1070 us
  waiting for transfers between devices  579 us (54%)
  matrix products  349 us (32%)
  other arithmetic  81.1 us (8%)
  local copies, waits for them, and re-layouts  43.3 us (4%)
  between operations  15 us (1%)
    unnamed x15, waiting for transfers between devices  318 us
    reshape x3, waiting for transfers between devices, step(): t.reshape(-1, *t.shape[2:])  261 us
    dot_general x5, matrix products, layer(): gate = jnp.dot(a, w['w_gate'], preferred_element_type=jnp.float32)  122 us
    dot_general x5, matrix products, layer(): up = jnp.dot(a, w['w_up'], preferred_element_type=jnp.float32)  113 us
    dot_general x5, matrix products, matmul(): jnp.dot(a, w, preferred_element_type=jnp.float32).astype(jnp.bfloat16)  113 us
    unnamed x5, other arithmetic  55.1 us
    unnamed x55, local copies, waits for them, and re-layouts  42.7 us
  transfers between devices with their start and end apart: 9, of which 7 were waited for; matrix products, arithmetic and copies ran while one was open for 26% of the time, Pallas kernels for 0%

commit v1 on v0

v1 whole, which is shorter than its diff:
```python
import jax
import jax.numpy as jnp
from jax import lax
from jax.sharding import PartitionSpec as P

NAMES = ("w_gate", "w_up", "w_down")


def matmul(a, w):
    return jnp.dot(a, w, preferred_element_type=jnp.float32).astype(jnp.bfloat16)


def normed(h):
    wide = h.astype(jnp.float32)
    scale = lax.rsqrt(jnp.mean(wide**2, -1, keepdims=True) + 1e-6)
    return (wide * scale).astype(jnp.bfloat16)


def layer(h, w):
    a = normed(h)
    gate = jnp.dot(a, w["w_gate"], preferred_element_type=jnp.float32)
    up = jnp.dot(a, w["w_up"], preferred_element_type=jnp.float32)
    return h + matmul((jax.nn.silu(gate) * up).astype(jnp.bfloat16), w["w_down"])


def adamw(w, m, v, g):
    m = 0.9 * m + 0.1 * g
    v = 0.95 * v + 0.05 * g * g
    step = m * lax.rsqrt(v + 1e-8) + 0.1 * w
    return (w - 0.02 * step).astype(jnp.bfloat16), m, v


def solution(mesh):
    def body(x, dy, *arrays):
        weights, m, v = (arrays[i : i + 3] for i in (0, 3, 6))
        x, dy = x[0], dy[0]
        layers = weights[0].shape[0]
        split = [dict(zip(NAMES, (w[n] for w in weights), strict=True)) for n in range(layers)]

        backs, h = [], x
        for n in range(layers):
            h, back = jax.vjp(layer, h, split[n])
            backs.append(back)
        me = lax.axis_index("dp")
        new = [[None] * layers for _ in NAMES]
        for n in reversed(range(layers)):
            dy, grads = backs[n](dy)
            for k in (2, 0, 1):
                g = lax.psum_scatter(grads[NAMES[k]], "dp", scatter_dimension=0, tiled=True)
                rows = g.shape[0]
                w = lax.dynamic_slice_in_dim(weights[k][n], me * rows, rows)
                w, mm, vv = adamw(w.astype(jnp.float32), m[k][n], v[k][n], g.astype(jnp.float32))
                new[k][n] = (lax.all_gather(w, "dp", axis=0, tiled=True), mm, vv)
        return tuple(jnp.stack([one[which] for one in new[k]]) for which in range(3) for k in range(len(NAMES)))

    whole, rows = P(None, None, None), P(None, "dp", None)
    return jax.shard_map(
        body,
        mesh=mesh,
        in_specs=(P(("rep", "dp")),) * 2 + (whole,) * 3 + (rows,) * 6,
        out_specs=(P("rep"),) * 3 + (P("rep", "dp"),) * 6,
        check_vma=False,
    )
```

time: 1080 us -> 1050 us (0.972)
  waiting for transfers between devices: 579 us -> 550 us
  matrix products: 349 us -> 372 us
  other arithmetic: 81.1 us -> 60.8 us
    all_gather x0 -> x6, waiting for transfers between devices: none -> 317 us  [body(): new[k][n] = (lax.all_gather(w, 'dp', axis=0, tiled=True), mm, vv)]
    unnamed x15 -> x14, waiting for transfers between devices: 318 us -> 2.35 us
    reshape x3 -> x0, waiting for transfers between devices: 261 us -> none  [step(): t.reshape(-1, *t.shape[2:])]
    reduce_scatter x0 -> x4, waiting for transfers between devices: none -> 230 us  [body(): g = lax.psum_scatter(grads[NAMES[k]], 'dp', scatter_dimension=0, tiled=True)]
    unnamed x5 -> x0, other arithmetic: 55.1 us -> none
    another operation x0 -> x6, other arithmetic: none -> 38.4 us  [body(): jnp.stack([one[which] for one in new[k]])]
    slice x0 -> x3, local copies, waits for them, and re-layouts: none -> 31.5 us  [the longest x2 21.1 us: body(): w[n]]
    unnamed x55 -> x30, local copies, waits for them, and re-layouts: 42.7 us -> 15.9 us
  transfers between devices with their start and end apart: 9 -> 12, of which waited for: 7 -> 10; matrix products, arithmetic and copies ran while one was open for 26% -> 26% of each run, Pallas kernels for 0% -> 0%
where the time goes in v1:
time: 1050 us
  waiting for transfers between devices  550 us (52%)
  matrix products  372 us (35%)
  other arithmetic  60.8 us (6%)
  local copies, waits for them, and re-layouts  47.4 us (5%)
  between operations  14.6 us (1%)
    all_gather x6, waiting for transfers between devices, body(): new[k][n] = (lax.all_gather(w, 'dp', axis=0, tiled=True), mm, vv)  317 us
    reduce_scatter x4, waiting for transfers between devices, body(): g = lax.psum_scatter(grads[NAMES[k]], 'dp', scatter_dimension=0, tiled=True)  230 us
    dot_general x5, matrix products, layer(): gate = jnp.dot(a, w['w_gate'], preferred_element_type=jnp.float32)  137 us
    dot_general x5, matrix products, layer(): up = jnp.dot(a, w['w_up'], preferred_element_type=jnp.float32)  125 us
    dot_general x5, matrix products, matmul(): jnp.dot(a, w, preferred_element_type=jnp.float32).astype(jnp.bfloat16)  110 us
    another operation x6, other arithmetic, body(): jnp.stack([one[which] for one in new[k]])  38.4 us
    slice x2, local copies, waits for them, and re-layouts, body(): w[n]  21.1 us
  transfers between devices with their start and end apart: 12, of which 10 were waited for; matrix products, arithmetic and copies ran while one was open for 26% of the time, Pallas kernels for 0%

profile of v1, /device:TPU:96, one launch (start us, length us, event | category | flops | bytes accessed | tf_op | source)
XLA Modules:
  0.0 1046.1 jit_solution(5318180352390465952)
XLA Ops:
  7.3 6.6 copy.22
  13.8 3.1 fusion.15
  16.9 21.9 %fusion.41 = f32[2048,3200]{1,0:T(8,128)} fusion(bf16[1,2048,1024]{2,1,0:T(8,128)(2,1)} %param.11, f32[2048]{0:T(1024)S(1)} %add_rsqrt_fusion, bf16[2,1024,3200]{2,1,0:T(8,128)(2,1)} %param.13), kind=kOutput, calls=%fused_computation.63 | convolution fusion | flops 13428064256 | bytes 36970496 | tf_op jit(solution)/shard_map/jvp()/dot_general | solution.py:21
  38.8 32.1 %multiply_convert_fusion.1 = (bf16[2048,3200]{1,0:T(8,128)(2,1)}, f32[2048,3200]{1,0:T(8,128)}) fusion(f32[2048,3200]{1,0:T(8,128)} %fusion.41, bf16[2,1024,3200]{2,1,0:T(8,128)(2,1)} %param.14, bf16[1,2048,1024]{2,1,0:T(8,128)(2,1)} %param.11, f32[2048]{0:T(1024)S(1)} %add_rsqrt_fusion), kind=kOutput, calls=%fused_computation.17 | convolution fusion | flops 13467385856 | bytes 76292096 | tf_op jit(solution)/shard_map/jvp()/dot_general | solution.py:22
  70.9 22.0 %fusion.19 = (f32[2048]{0:T(1024)S(1)}, bf16[2048,1024]{0,1:T(8,128)(2,1)}) fusion(bf16[2048,3200]{1,0:T(8,128)(2,1)} %get-tuple-element.33, bf16[2,3200,1024]{2,1,0:T(8,128)(2,1)} %param.15, bf16[1,2048,1024]{1,2,0:T(8,128)(2,1)} %copy.22), kind=kOutput, calls=%fused_computation.40 | convolution fusion | flops 13432256512 | bytes 28057600 | tf_op jit(solution)/shard_map/jvp()/dot_general | solution.py:10
  92.9 0.6 copy-done.10
  93.5 21.1 %convolution_convert_fusion.1 = bf16[2048,3200]{1,0:T(8,128)(2,1)} fusion(bf16[1,2048,1024]{2,1,0:T(8,128)(2,1)} %param.12, bf16[2,3200,1024]{2,1,0:T(8,128)(2,1)} %param.15), kind=kOutput, calls=%fused_computation.23 | convolution fusion | flops 13428326400 | bytes 23855104 | tf_op jit(solution)/shard_map/transpose(jvp())/dot_general | solution.py:10
  114.6 20.7 %fusion.28 = f32[2048,3200]{1,0:T(8,128)} fusion(bf16[2048,1024]{0,1:T(8,128)(2,1)S(1)} %copy-done.2, f32[2048]{0:T(1024)S(1)} %fusion.102, bf16[2,1024,3200]{2,1,0:T(8,128)(2,1)} %param.14), kind=kOutput, calls=%fused_computation.50 | convolution fusion | flops 13428064256 | bytes 36970496 | tf_op jit(solution)/shard_map/jvp()/dot_general | solution.py:22
  135.3 39.0 %fusion.2 = (bf16[2048,3200]{1,0:T(8,128)(2,1)}, f32[2048,3200]{1,0:T(8,128)}) fusion(f32[2048,3200]{1,0:T(8,128)} %fusion.28, bf16[2048,3200]{1,0:T(8,128)(2,1)} %convolution_convert_fusion.1, bf16[2,1024,3200]{2,1,0:T(8,128)(2,1)} %param.13, bf16[2048,1024]{0,1:T(8,128)(2,1)} %get-tuple-element.36, f32[2048]{0:T(1024)S(1)} %fusion.102), kind=kOutput, calls=%fused_computation.8 | convolution fusion | flops 13506707456 | bytes 89399296 | tf_op jit(solution)/shard_map/jvp()/dot_general | solution.py:21
  174.3 25.7 %fusion.25 = bf16[3200,1024]{1,0:T(8,128)(2,1)} fusion(f32[2048,3200]{1,0:T(8,128)} %fusion.28, bf16[1,2048,1024]{2,1,0:T(8,128)(2,1)} %param.12, f32[2048,3200]{1,0:T(8,128)} %get-tuple-element.38), kind=kOutput, calls=%fused_computation.45 | convolution fusion | flops 13464371200 | bytes 63176704 | tf_op jit(solution)/shard_map/transpose(jvp())/dot_general | solution.py:10
  200.1 0.1 reduce-scatter.19.cloned.1.call-start
  200.2 6.7 copy.23
  206.8 22.6 %fusion.12 = bf16[2048,1024]{0,1:T(8,128)(2,1)} fusion(bf16[2048,3200]{1,0:T(8,128)(2,1)} %convolution_convert_fusion.1, bf16[2,1024,3200]{2,1,0:T(8,128)(2,1)} %param.14, f32[2048,3200]{1,0:T(8,128)} %get-tuple-element.38), kind=kOutput, calls=%fused_computation.21 | convolution fusion | flops 13461094400 | bytes 50069504 | tf_op jit(solution)/shard_map/transpose(jvp())/dot_general | solution.py:22
  229.5 23.0 %fusion.21 = (f32[2048]{0:T(1024)S(1)}, bf16[2048,1024]{0,1:T(8,128)(2,1)}) fusion(bf16[2048,1024]{0,1:T(8,128)(2,1)} %get-tuple-element.36, bf16[2048,1024]{0,1:T(8,128)(2,1)} %fusion.12, bf16[2048,3200]{1,0:T(8,128)(2,1)} %get-tuple-element.37, bf16[2,1024,3200]{2,1,0:T(8,128)(2,1)} %param.13), kind=kOutput, calls=%fused_computation.42 | convolution fusion | flops 13432256512 | bytes 32251904 | tf_op jit(solution)/shard_map/transpose(jvp())/dot_general | solution.py:21
  252.5 5.3 fusion.45
  257.8 2.0 copy-done.3
  259.8 19.4 %convolution_convert_fusion.2 = bf16[3200,1024]{1,0:T(8,128)(2,1)} fusion(bf16[2048,3200]{1,0:T(8,128)(2,1)} %get-tuple-element.33, bf16[2048,1024]{0,1:T(8,128)(2,1)S(1)} %fusion.45), kind=kOutput, calls=%fused_computation.48 | convolution fusion | flops 13425049600 | bytes 23855104 | tf_op jit(solution)/shard_map/transpose(jvp())/dot_general | solution.py:10
  279.4 25.5 %fusion.26 = bf16[1024,3200]{1,0:T(8,128)(2,1)} fusion(bf16[2048,3200]{1,0:T(8,128)(2,1)} %convolution_convert_fusion.1, bf16[2048,1024]{0,1:T(8,128)(2,1)} %get-tuple-element.36, f32[2048]{0:T(1024)S(1)} %copy-done.9, f32[2048,3200]{1,0:T(8,128)} %get-tuple-element.38), kind=kOutput, calls=%fused_computation.46 | convolution fusion | flops 13470662656 | bytes 50077696 | tf_op jit(solution)/shard_map/transpose(jvp())/dot_general | solution.py:22
  305.1 21.6 %convolution_convert_fusion = bf16[2048,3200]{1,0:T(8,128)(2,1)} fusion(bf16[2048,1024]{0,1:T(8,128)(2,1)} %copy-done.3, bf16[2,3200,1024]{2,1,0:T(8,128)(2,1)} %param.15), kind=kOutput, calls=%fused_computation.22 | convolution fusion | flops 13428326400 | bytes 23855104 | tf_op jit(solution)/shard_map/transpose(jvp())/dot_general | solution.py:10
  326.6 24.3 %fusion.27 = bf16[1024,3200]{1,0:T(8,128)(2,1)} fusion(bf16[2048,3200]{1,0:T(8,128)(2,1)} %convolution_convert_fusion, f32[2048,3200]{1,0:T(8,128)} %fusion.41, bf16[1,2048,1024]{1,2,0:T(8,128)(2,1)S(1)} %copy-done.1, f32[2048]{0:T(1024)S(1)} %copy-done.13), kind=kOutput, calls=%fused_computation.47 | convolution fusion | flops 13470662656 | bytes 50077696 | tf_op jit(solution)/shard_map/transpose(jvp())/dot_general | solution.py:22
  351.0 21.1 %convolution_convert_fusion.3 = bf16[1024,3200]{1,0:T(8,128)(2,1)} fusion(bf16[2048,3200]{1,0:T(8,128)(2,1)} %get-tuple-element.37, bf16[2048,1024]{0,1:T(8,128)(2,1)} %get-tuple-element.36, f32[2048]{0:T(1024)S(1)} %copy-done.9), kind=kOutput, calls=%fused_computation.49 | convolution fusion | flops 13428064256 | bytes 23863296 | tf_op jit(solution)/shard_map/transpose(jvp())/dot_general | solution.py:21
  372.2 0.1 reduce-scatter.11.cloned.1.call-start
  372.3 32.5 %fusion.22 = bf16[1024,3200]{1,0:T(8,128)(2,1)} fusion(f32[2048,3200]{1,0:T(8,128)} %fusion.41, f32[2048,3200]{1,0:T(8,128)} %get-tuple-element.34, bf16[2048,3200]{1,0:T(8,128)(2,1)} %convolution_convert_fusion, bf16[1,2048,1024]{1,2,0:T(8,128)(2,1)} %copy.22, f32[2048]{0:T(1024)S(1)} %copy-done.13), kind=kOutput, calls=%fused_computation.44 | convolution fusion | flops 13503430656 | bytes 76292096 | tf_op jit(solution)/shard_map/transpose(jvp())/dot_general | solution.py:21
  404.9 10.7 %fusion.117 = (bf16[1,3200,1024]{2,1,0:T(8,128)(2,1)}, bf16[1,3200,1024]{2,1,0:T(8,128)(2,1)}) fusion(bf16[2,3200,1024]{2,1,0:T(8,128)(2,1)} %param.15), kind=kLoop, calls=%fused_computation.158 | loop fusion | bytes 26214400 | tf_op jit(solution)/shard_map/slice | solution.py:38
  415.6 4.3 fusion.80
  420.0 0.7 all-gather.17.cloned.1.call-update
  420.8 10.4 fusion.118
  431.2 7.7 reduce-scatter.17.cloned.1.call-done
  438.9 79.3 %reduce-scatter.15.cloned.1.call-done = bf16[64,3200]{1,0:T(8,128)(2,1)} async-done(((bf16[1024,3200]{1,0:T(8,128)(2,1)}), bf16[64,3200]{1,0:T(8,128)(2,1)}) %reduce-scatter.15.cloned.1.call-update) | async-done | bytes 409616 | tf_op jit(solution)/shard_map/reduce_scatter | solution.py:49
  518.2 4.8 fusion.74
  523.2 0.6 all-gather.13.cloned.1.call-update
  523.8 10.4 fusion.119
  534.2 63.4 %reduce-scatter.13.cloned.1.call-done = bf16[64,3200]{1,0:T(8,128)(2,1)} async-done(((bf16[1024,3200]{1,0:T(8,128)(2,1)}), bf16[64,3200]{1,0:T(8,128)(2,1)}) %reduce-scatter.13.cloned.1.call-update) | async-done | bytes 409616 | tf_op jit(solution)/shard_map/reduce_scatter | solution.py:49
  597.6 80.0 %reduce-scatter.11.cloned.1.call-done = bf16[64,3200]{1,0:T(8,128)(2,1)} async-done(((bf16[1024,3200]{1,0:T(8,128)(2,1)}), bf16[64,3200]{1,0:T(8,128)(2,1)}) %reduce-scatter.11.cloned.1.call-update) | async-done | bytes 409616 | tf_op jit(solution)/shard_map/reduce_scatter | solution.py:49
  677.6 4.8 fusion.68
  682.6 0.6 all-gather.9.cloned.1.call-update
  683.2 1.9 pad_maximum_fusion.5
  685.1 4.0 pad_maximum_fusion.4
  689.1 1.9 pad_maximum_fusion.3
  691.1 44.9 %all-gather.15.cloned.1.call-done = bf16[3200,1024]{1,0:T(8,128)(2,1)} async-done(((bf16[200,1024]{1,0:T(8,128)(2,1)}), bf16[3200,1024]{1,0:T(8,128)(2,1)}) %all-gather.15.cloned.1.call-update) | async-done | bytes 6553616 | tf_op jit(solution)/shard_map/all_gather | solution.py:53
  736.0 58.7 %all-gather.17.cloned.1.call-done = bf16[3200,1024]{1,0:T(8,128)(2,1)} async-done(((bf16[200,1024]{1,0:T(8,128)(2,1)}), bf16[3200,1024]{1,0:T(8,128)(2,1)}) %all-gather.17.cloned.1.call-update) | async-done | bytes 6553616 | tf_op jit(solution)/shard_map/all_gather | solution.py:53
  794.6 10.8 %pad_maximum_fusion.2 = bf16[2,3200,1024]{2,1,0:T(8,128)(2,1)} fusion(bf16[1,3200,1024]{2,1,0:T(8,128)(2,1)} %bitcast.184, bf16[1,3200,1024]{2,1,0:T(8,128)(2,1)} %bitcast.183), kind=kLoop, calls=%fused_computation.31 | loop fusion | flops 6553600 | bytes 26214400 | tf_op jit(solution)/shard_map/stack | solution.py:54
  805.4 47.9 %all-gather.11.cloned.1.call-done = bf16[1024,3200]{1,0:T(8,128)(2,1)} async-done(((bf16[64,3200]{1,0:T(8,128)(2,1)}), bf16[1024,3200]{1,0:T(8,128)(2,1)}) %all-gather.11.cloned.1.call-update) | async-done | bytes 6553616 | tf_op jit(solution)/shard_map/all_gather | solution.py:53
  853.3 58.5 %all-gather.13.cloned.1.call-done = bf16[1024,3200]{1,0:T(8,128)(2,1)} async-done(((bf16[64,3200]{1,0:T(8,128)(2,1)}), bf16[1024,3200]{1,0:T(8,128)(2,1)}) %all-gather.13.cloned.1.call-update) | async-done | bytes 6553616 | tf_op jit(solution)/shard_map/all_gather | solution.py:53
  911.9 9.9 pad_maximum_fusion.1
  921.8 48.8 %all-gather.7.cloned.1.call-done = bf16[1024,3200]{1,0:T(8,128)(2,1)} async-done(((bf16[64,3200]{1,0:T(8,128)(2,1)}), bf16[1024,3200]{1,0:T(8,128)(2,1)}) %all-gather.7.cloned.1.call-update) | async-done | bytes 6553616 | tf_op jit(solution)/shard_map/all_gather | solution.py:53
  970.5 58.5 %all-gather.9.cloned.1.call-done = bf16[1024,3200]{1,0:T(8,128)(2,1)} async-done(((bf16[64,3200]{1,0:T(8,128)(2,1)}), bf16[1024,3200]{1,0:T(8,128)(2,1)}) %all-gather.9.cloned.1.call-update) | async-done | bytes 6553616 | tf_op jit(solution)/shard_map/all_gather | solution.py:53
  1029.1 9.9 pad_maximum_fusion
  (50 shorter events, 1.2 us)
Async XLA Ops:
  7.2 408.4 %reduce-scatter.21.cloned.1.call-start = ((), (), s32[]{:S(2)}) async-start(), calls=%async_computation.17 | async-start | bytes 6963200
  16.9 21.9 %copy-start.12 = (f32[2048]{0:T(1024)}, f32[2048]{0:T(1024)S(1)}, u32[]{:S(2)}) copy-start(f32[2048]{0:T(1024)S(1)} %add_rsqrt_fusion) | copy-start | bytes 24580
  92.9 0.6 copy-start.10
  93.5 41.8 %copy-start.8 = (f32[2048]{0:T(1024)}, f32[2048]{0:T(1024)S(1)}, u32[]{:S(2)}) copy-start(f32[2048]{0:T(1024)S(1)} %fusion.102) | copy-start | bytes 24580
  93.5 21.2 %copy-start.2 = (bf16[2048,1024]{0,1:T(8,128)(2,1)S(1)}, bf16[2048,1024]{0,1:T(8,128)(2,1)}, u32[]{:S(2)}) copy-start(bf16[2048,1024]{0,1:T(8,128)(2,1)} %get-tuple-element.36) | copy-start | bytes 12582916
  200.1 215.5 %reduce-scatter.19.cloned.1.call-start = ((), (), s32[]{:S(2)}) async-start(), calls=%async_computation.16 | async-start | bytes 6963200
  229.5 23.0 %copy-start.11 = (f32[2048]{0:T(1024)S(1)}, f32[2048]{0:T(1024)}, u32[]{:S(2)}) copy-start(f32[2048]{0:T(1024)} %copy-done.10) | copy-start | bytes 24580
  229.5 23.0 %copy-start = (bf16[1,2048,1024]{1,2,0:T(8,128)(2,1)S(1)}, bf16[1,2048,1024]{1,2,0:T(8,128)(2,1)}, u32[]{:S(2)}) copy-start(bf16[1,2048,1024]{1,2,0:T(8,128)(2,1)} %copy.23) | copy-start | bytes 12582916
  229.5 23.0 %copy-start.9 = (f32[2048]{0:T(1024)S(1)}, f32[2048]{0:T(1024)}, u32[]{:S(2)}) copy-start(f32[2048]{0:T(1024)} %copy-done.8) | copy-start | bytes 24580
  257.8 2.0 copy-start.3
  279.3 159.6 %reduce-scatter.17.cloned.1.call-start = ((), (), s32[]{:S(2)}) async-start(), calls=%async_computation.12 | async-start | bytes 6963200 | tf_op jit(solution)/shard_map/reduce_scatter | solution.py:49
  305.0 21.7 %copy-start.13 = (f32[2048]{0:T(1024)S(1)}, f32[2048]{0:T(1024)}, u32[]{:S(2)}) copy-start(f32[2048]{0:T(1024)} %copy-done.12) | copy-start | bytes 24580
  305.0 213.2 %reduce-scatter.15.cloned.1.call-start = ((), (), s32[]{:S(2)}) async-start(), calls=%async_computation.10 | async-start | bytes 6963200 | tf_op jit(solution)/shard_map/reduce_scatter | solution.py:49
  305.0 21.6 %copy-start.1 = (bf16[1,2048,1024]{1,2,0:T(8,128)(2,1)S(1)}, bf16[1,2048,1024]{1,2,0:T(8,128)(2,1)}, u32[]{:S(2)}) copy-start(bf16[1,2048,1024]{1,2,0:T(8,128)(2,1)} %copy.22) | copy-start | bytes 12582916
  350.9 246.7 %reduce-scatter.13.cloned.1.call-start = ((), (), s32[]{:S(2)}) async-start(), calls=%async_computation.8 | async-start | bytes 6963200 | tf_op jit(solution)/shard_map/reduce_scatter | solution.py:49
  372.2 305.4 %reduce-scatter.11.cloned.1.call-start = ((), (), s32[]{:S(2)}) async-start(), calls=%async_computation.6 | async-start | bytes 6963200 | tf_op jit(solution)/shard_map/reduce_scatter | solution.py:49
  404.8 331.2 %all-gather.15.cloned.1.call-start = ((), (), s32[]{:S(2)}) async-start(), calls=%async_computation.14 | async-start | bytes 6963200 | tf_op jit(solution)/shard_map/all_gather | solution.py:53
  419.9 374.7 %all-gather.17.cloned.1.call-start = ((), (), s32[]{:S(2)}) async-start(), calls=%async_computation.15 | async-start | bytes 6963200 | tf_op jit(solution)/shard_map/all_gather | solution.py:53
  420.8 432.6 %all-gather.11.cloned.1.call-start = ((), (), s32[]{:S(2)}) async-start(), calls=%async_computation.11 | async-start | bytes 6963200 | tf_op jit(solution)/shard_map/all_gather | solution.py:53
  523.1 388.8 %all-gather.13.cloned.1.call-start = ((), (), s32[]{:S(2)}) async-start(), calls=%async_computation.13 | async-start | bytes 6963200 | tf_op jit(solution)/shard_map/all_gather | solution.py:53
  523.7 446.8 %all-gather.7.cloned.1.call-start = ((), (), s32[]{:S(2)}) async-start(), calls=%async_computation.7 | async-start | bytes 6963200 | tf_op jit(solution)/shard_map/all_gather | solution.py:53
  682.5 346.5 %all-gather.9.cloned.1.call-start = ((), (), s32[]{:S(2)}) async-start(), calls=%async_computation.9 | async-start | bytes 6963200 | tf_op jit(solution)/shard_map/all_gather | solution.py:53
  683.2 6.0 copy-start.4
  683.2 6.0 copy-start.5
  683.2 6.0 copy-start.6
  683.2 5.9 copy-start.7
Sparse Core Ops, SparseCore 0:
  200.2 79.5 reduce-scatter.20
  283.0 76.2 reduce-scatter.18
  362.6 76.2 reduce-scatter.16
  442.0 76.1 reduce-scatter.14
  521.3 76.2 reduce-scatter.12
  601.3 76.2 reduce-scatter.10
  679.6 56.2 all-gather.14
  738.0 56.6 all-gather.16
  796.7 56.6 all-gather.10
  855.2 56.6 all-gather.12
  913.9 56.6 all-gather.6
  972.4 56.6 all-gather.8

commit v2 on v1

v2 whole, which is shorter than its diff:
```python
import functools
import math

import jax
import jax.numpy as jnp
from jax import lax
from jax.experimental import pallas as pl
from jax.experimental.pallas import tpu as pltpu
from jax.sharding import PartitionSpec as P

BF, F32 = jnp.bfloat16, jnp.float32
MESH = pl.DeviceIdType.MESH
SIDE = 4
KINDS = 4
BLOCKS = 5
LANES = 128
SLOTS = 6
ANY = pl.BlockSpec(memory_space=pl.ANY)


def dot(a, b, da, db):
    return lax.dot_general(a, b, (((da,), (db,)), ((), ())), preferred_element_type=F32)


def normed(wide):
    return (wide * lax.rsqrt(jnp.mean(wide * wide, -1, keepdims=True) + 1e-6)).astype(BF)


def forward_kernel(x_ref, wg_ref, wu_ref, wd_ref, a0_ref, h1_ref, a1_ref, acc, *, rows):
    b = pl.program_id(0)

    def part(t, _):
        at = pl.ds(pl.multiple_of(t * rows, rows), rows)

        @pl.when(b == 0)
        def _():
            a0_ref[at, :] = normed(x_ref[at, :].astype(F32))

        a = a0_ref[at, :]
        gate = dot(a, wg_ref[...], 1, 0)
        up = dot(a, wu_ref[...], 1, 0)
        hidden = (gate * jax.nn.sigmoid(gate) * up).astype(BF)
        more = dot(hidden, wd_ref[...], 1, 0)

        @pl.when(b == 0)
        def _():
            acc[at, :] = more

        @pl.when(b > 0)
        def _():
            acc[at, :] = acc[at, :] + more

        @pl.when(b == pl.num_programs(0) - 1)
        def _():
            h = x_ref[at, :] + acc[at, :].astype(BF)
            h1_ref[at, :] = h
            a1_ref[at, :] = normed(h.astype(F32))

        return 0

    lax.fori_loop(0, x_ref.shape[0] // rows, part, 0)


def first_layer(x, wg, wu, wd):
    n, d = x.shape
    f = wg.shape[2] // BLOCKS
    whole = pl.BlockSpec((n, d), lambda b: (0, 0))
    return pl.pallas_call(
        functools.partial(forward_kernel, rows=256),
        grid=(BLOCKS,),
        out_shape=[jax.ShapeDtypeStruct((n, d), BF)] * 3,
        in_specs=[
            whole,
            pl.BlockSpec((None, d, f), lambda b: (0, 0, b)),
            pl.BlockSpec((None, d, f), lambda b: (0, 0, b)),
            pl.BlockSpec((None, f, d), lambda b: (0, b, 0)),
        ],
        out_specs=[whole] * 3,
        scratch_shapes=[pltpu.VMEM((n, d), F32)],
        compiler_params=pltpu.CompilerParams(vmem_limit_bytes=60 * 2**20),
        name="first_layer",
    )(x, wg, wu, wd)


def step_kernel(a0_h, a1_h, h1_h, dy_h, wg_h, wu_h, wd_h, mg_h, mu_h, md_h, vg_h, vu_h, vd_h,
                og_h, ou_h, od_h, omg_h, omu_h, omd_h, ovg_h, ovu_h, ovd_h, dgs_h, dus_h,
                a, dy, wg, wu, wd, hid, dg, du, acc, dwg, dwd,
                r1, r2, r3, t3, q1, q2, q3,
                cw, cm, cv, nw, nm, nv, ew, em, ev, fw, fm, fv,
                ss, rs, lw, la, lb, ls, lp, lo, *, layers, units, ring, dring):
    n, d = a.shape
    f = wg.shape[1]
    rows_g = d // (SIDE * SIDE)
    rows_d = f * BLOCKS // (SIDE * SIDE)
    sub_g, sub_d = rows_g // KINDS, rows_d // BLOCKS
    per_layer = units // layers
    me = lax.axis_index("dp")
    mx, my = me // SIDE, me % SIDE
    wrap = lambda v: lax.rem(v + 2 * SIDE, SIDE)
    dev = lambda x, y: {"dp": wrap(x) * SIDE + wrap(y)}

    barrier = pltpu.get_barrier_semaphore()
    for x, y in ((mx + 1, my), (mx - 1, my), (mx, my + 1), (mx, my - 1)):
        pl.semaphore_signal(barrier, inc=1, device_id=dev(x, y), device_id_type=MESH)

    def load(src, dst, sem):
        return pltpu.make_async_copy(src, dst, sem)

    def weights(layer, b):
        cols = pl.ds(pl.multiple_of(b * f, LANES), f)
        rows = pl.ds(pl.multiple_of(b * f, 8), f)
        return (load(wg_h.at[layer, :, cols], wg, lw.at[0]), load(wu_h.at[layer, :, cols], wu, lw.at[1]),
                load(wd_h.at[layer, rows, :], wd, lw.at[2]))

    def states(src):
        return load(src, a, la.at[0])

    def saved(b):
        cols = pl.ds(pl.multiple_of(b * f, LANES), f)
        return (load(dg, dgs_h.at[:, cols], ls.at[0]), load(du, dus_h.at[:, cols], ls.at[1]))

    def back(b):
        cols = pl.ds(pl.multiple_of(b * f, LANES), f)
        return (load(dgs_h.at[:, cols], dg, lb.at[0]), load(dus_h.at[:, cols], du, lb.at[1]))

    load_dy = load(dy_h, dy, la.at[1])
    states(a1_h).start()
    load_dy.start()
    for c in weights(layers - 1, 0):
        c.start()
    pl.semaphore_wait(barrier, 4)

    TT = 256

    def tokens(t):
        return pl.ds(pl.multiple_of(t * TT, TT), TT)

    def gradient_columns(which, slot):
        quarter = d // SIDE

        def part(r, _):
            cols = pl.ds(pl.multiple_of(r * quarter, LANES), quarter)
            g = dot(a[:, cols], which[...], 0, 0).astype(BF)
            g = g.reshape(SIDE, KINDS, sub_g, f)
            for i in range(KINDS):
                for c in range(f // LANES):
                    dwg[slot, i, r, :, c * sub_g : (c + 1) * sub_g, :] = g[:, i, :, c * LANES : (c + 1) * LANES]
            return 0

        lax.fori_loop(0, SIDE, part, 0)

    def gradient_rows(b, first):
        cols_k = d // KINDS

        def part(i, _):
            cols = pl.ds(pl.multiple_of(i * cols_k, LANES), cols_k)
            g = dot(hid[...], dy[:, cols], 0, 0).astype(BF)
            for k in range(f // sub_d):
                unit = b * (f // sub_d) + k
                owner, j = unit // BLOCKS, unit % BLOCKS
                slot = lax.rem(first + j, dring)
                for c in range(cols_k // LANES):
                    dwd[slot, i, owner // SIDE, owner % SIDE, c * sub_d : (c + 1) * sub_d, :] = (
                        g[k * sub_d : (k + 1) * sub_d, c * LANES : (c + 1) * LANES])
            return 0

        lax.fori_loop(0, KINDS, part, 0)

    def hidden_block(layer, b, slot):
        for c in weights(layer, b):
            c.wait()

        @pl.when(b == 0)
        def _():
            states(a0_h).wait()

            @pl.when(layer == layers - 1)
            def _():
                load_dy.wait()

        def part(t, _):
            at = tokens(t)
            gate = dot(a[at, :], wg[...], 1, 0)
            up = dot(a[at, :], wu[...], 1, 0)
            back = dot(dy[at, :], wd[...], 1, 1).astype(BF).astype(F32)
            s = jax.nn.sigmoid(gate)
            silu = gate * s
            hid[at, :] = (silu * up).astype(BF)
            du[at, :] = (back * silu).astype(BF)
            dg[at, :] = (back * up * (s + silu * (1 - s))).astype(BF)
            return 0

        lax.fori_loop(0, n // TT, part, 0)

        @pl.when(layer > 0)
        def _():
            for c in saved(b):
                c.start()

        @pl.when(b < BLOCKS - 1)
        def _():
            for c in weights(layer, b + 1):
                c.start()

        @pl.when((b == BLOCKS - 1) & (layer > 0))
        def _():
            for c in weights(layer, 0)[:2]:
                c.start()

        gradient_columns(dg, slot)

    def hidden_rest(layer, b, slot, first):
        gradient_columns(du, slot)
        gradient_rows(b, first)

        @pl.when(layer > 0)
        def _():
            for c in saved(b):
                c.wait()

            @pl.when(b == BLOCKS - 1)
            def _():
                for c in back(0):
                    c.start()
                states(h1_h).start()

    def states_back(layer, q):
        for c in weights(layer, q)[:2]:
            c.wait()
        for c in back(q):
            c.wait()

        def part(t, _):
            at = tokens(t)
            more = dot(dg[at, :], wg[...], 1, 1) + dot(du[at, :], wu[...], 1, 1)

            @pl.when(q == 0)
            def _():
                acc[at, :] = more

            @pl.when(q > 0)
            def _():
                acc[at, :] = acc[at, :] + more

            return 0

        lax.fori_loop(0, n // TT, part, 0)

        @pl.when(q < BLOCKS - 1)
        def _():
            for c in weights(layer, q + 1)[:2]:
                c.start()
            for c in back(q + 1):
                c.start()

        @pl.when(q == BLOCKS - 1)
        def _():
            for c in weights(layer - 1, 0):
                c.start()
            states(h1_h).wait()

            def part(t, _):
                at = pl.ds(pl.multiple_of(t * 64, 64), 64)
                wide = a[at, :].astype(F32)
                scale = lax.rsqrt(jnp.mean(wide * wide, -1, keepdims=True) + 1e-6)
                by = acc[at, :].astype(BF).astype(F32)
                along = jnp.mean(by * wide, -1, keepdims=True)
                more = by * scale - wide * (scale * scale * scale * along)
                dy[at, :] = (dy[at, :].astype(F32) + more.astype(BF).astype(F32)).astype(BF)
                return 0

            lax.fori_loop(0, n // 64, part, 0)
            states(a0_h).start()

    def place(u):
        layer = layers - 1 - u // per_layer
        k = lax.rem(u, per_layer)
        down = k >= 2 * BLOCKS
        return layer, jnp.where(down, 2, lax.rem(k, 2)), jnp.where(down, k - 2 * BLOCKS, k // 2), k

    def dring_slot(u):
        return lax.rem((u // per_layer) * BLOCKS + lax.rem(u, per_layer) - 2 * BLOCKS + dring, dring)

    def steps(i):
        s = 1 - 2 * (i % 2)
        xs, ys = (dev(mx + s, my), dev(mx - s, my)), (dev(mx, my + s), dev(mx, my - s))
        return (*xs, *ys, mx, my, s) if i < 2 else (*ys, *xs, my, mx, s)

    def rcopy(src, dst, u, i, k, to):
        n_ = lax.rem(u, SLOTS)
        return pltpu.make_async_remote_copy(
            src_ref=src, dst_ref=dst, send_sem=ss.at[n_, i, k], recv_sem=rs.at[n_, i, k], device_id=to, device_id_type=MESH)

    def own(u, i, p):
        g, dn = dwg.at[lax.rem(u, ring), i], dwd.at[dring_slot(u), i]
        return tuple(w.at[p] if i < 2 else w.at[:, p] for w in (g, dn))

    def on_own(u, do):
        k = lax.rem(u, per_layer)
        pl.when(k < 2 * BLOCKS)(lambda: do(0))
        pl.when(k >= 2 * BLOCKS)(lambda: do(1))

    def s0_copies(u, i, which):
        ahead, behind, _, _, pf, _, s = steps(i)
        n_ = lax.rem(u, SLOTS)
        return (rcopy(own(u, i, wrap(pf + 2))[which], r1.at[n_, i], u, i, 0, ahead),
                rcopy(own(u, i, wrap(pf - s))[which], r2.at[n_, i], u, i, 1, behind))

    def s1_copy(u, i):
        ahead = steps(i)[0]
        n_ = lax.rem(u, SLOTS)
        return rcopy(r1.at[n_, i], r3.at[n_, i], u, i, 2, ahead)

    def s2_copies(u, i):
        _, _, ahead, behind, _, ps, s = steps(i)
        n_ = lax.rem(u, SLOTS)
        return (rcopy(r3.at[n_, i, wrap(ps + 2)], q1.at[n_, i], u, i, 3, ahead),
                rcopy(r3.at[n_, i, wrap(ps - s)], q2.at[n_, i], u, i, 4, behind))

    def s3_copy(u, i):
        ahead = steps(i)[2]
        n_ = lax.rem(u, SLOTS)
        return rcopy(q1.at[n_, i], q3.at[n_, i], u, i, 5, ahead)

    def state_copies(u):
        layer, _, j, _ = place(u)
        z = lax.rem(u, 2)
        cols = pl.ds(pl.multiple_of(j * f, LANES), f)
        rows = pl.ds(pl.multiple_of(me * rows_d + j * sub_d, 8), sub_d)
        mine = pl.ds(pl.multiple_of(j * sub_d, 8), sub_d)
        first = pl.ds(pl.multiple_of(me * rows_g, 8), rows_g)
        ins = tuple(
            (load(w.at[layer, first, cols], cw.at[z], lp.at[z, 0]), load(m.at[layer, :, cols], cm.at[z], lp.at[z, 1]),
             load(v.at[layer, :, cols], cv.at[z], lp.at[z, 2]))
            for w, m, v in ((wg_h, mg_h, vg_h), (wu_h, mu_h, vu_h))
        ) + ((load(wd_h.at[layer, rows, :], ew.at[z], lp.at[z, 0]), load(md_h.at[layer, mine, :], em.at[z], lp.at[z, 1]),
              load(vd_h.at[layer, mine, :], ev.at[z], lp.at[z, 2])),)
        outs = tuple(
            (load(nw.at[z], w.at[layer, mx, my, :, cols], lo.at[z, 0]), load(nm.at[z], m.at[layer, :, cols], lo.at[z, 1]),
             load(nv.at[z], v.at[layer, :, cols], lo.at[z, 2]))
            for w, m, v in ((og_h, omg_h, ovg_h), (ou_h, omu_h, ovu_h))
        ) + ((load(fw.at[z], od_h.at[layer, mx, my, mine, :], lo.at[z, 0]), load(fm.at[z], omd_h.at[layer, mine, :], lo.at[z, 1]),
              load(fv.at[z], ovd_h.at[layer, mine, :], lo.at[z, 2])),)
        return ins, outs

    def on_matrix(u, do):
        k = lax.rem(u, per_layer)
        down = k >= 2 * BLOCKS
        for which, test in enumerate((~down & (lax.rem(k, 2) == 0), ~down & (lax.rem(k, 2) == 1), down)):
            pl.when(test)(functools.partial(do, which))

    def out_at(u, i, which):
        layer, _, j, _ = place(u)
        if which < 2:
            cols = pl.ds(pl.multiple_of(j * f, LANES), f)
            return lambda x, y: (og_h, ou_h)[which].at[layer, x, y, pl.ds(i * sub_g, sub_g), cols]
        rows = pl.ds(pl.multiple_of(j * sub_d, 8), sub_d)
        wide = d // KINDS
        return lambda x, y: od_h.at[layer, x, y, rows, pl.ds(i * wide, wide)]

    def new_block(u, i, which):
        z = lax.rem(u, 2)
        wide = d // KINDS
        return nw.at[z, pl.ds(i * sub_g, sub_g), :] if which < 2 else fw.at[z, :, pl.ds(i * wide, wide)]

    def s4_copies(u, i, which):
        _, _, ahead, behind, _, _, _ = steps(i)
        dst = out_at(u, i, which)(mx, my)
        src = new_block(u, i, which)
        return (rcopy(src, dst, u, i, 6, ahead), rcopy(src, dst, u, i, 7, behind))

    def s5_copy(u, i, which):
        _, _, ahead, _, pf, ps, s = steps(i)
        at = out_at(u, i, which)
        src = at(pf, wrap(ps - s)) if i < 2 else at(wrap(ps - s), pf)
        return rcopy(src, src, u, i, 8, ahead)

    every = pl.ds(0, SIDE)

    def s6_copies(u, i, which):
        ahead, behind, _, _, pf, _, _ = steps(i)
        at = out_at(u, i, which)
        src = at(pf, every) if i < 2 else at(every, pf)
        return (rcopy(src, src, u, i, 9, ahead), rcopy(src, src, u, i, 10, behind))

    def s7_copy(u, i, which):
        ahead, _, _, _, pf, _, s = steps(i)
        at = out_at(u, i, which)
        p = wrap(pf - s)
        src = at(p, every) if i < 2 else at(every, p)
        return rcopy(src, src, u, i, 11, ahead)

    def stage0(u):
        def do(which):
            for i in range(KINDS):
                for c in s0_copies(u, i, which):
                    c.start()
        on_own(u, do)

    def stage1(u):
        n_ = lax.rem(u, SLOTS)

        def do(which):
            for i in range(KINDS):
                _, _, _, _, pf, _, s = steps(i)
                s0_copies(u, i, which)[0].wait()
                mine = own(u, i, wrap(pf + s))[which]
                r1[n_, i] = (r1[n_, i].astype(F32) + mine[...].astype(F32)).astype(BF)
                s1_copy(u, i).start()
        on_own(u, do)

    def stage2(u):
        n_ = lax.rem(u, SLOTS)

        def do(which):
            for i in range(KINDS):
                _, _, _, _, pf, ps, s = steps(i)
                s0_copies(u, i, which)[1].wait()
                s1_copy(u, i).wait()
                mine = own(u, i, pf)[which]
                for k in (2, -s, s, 0):
                    p = wrap(ps + k)
                    total = r2[n_, i, p].astype(F32) + r3[n_, i, p].astype(F32) + mine[p].astype(F32)
                    if k in (2, -s):
                        r3[n_, i, p] = total.astype(BF)
                    else:
                        t3[n_, i, 0 if k else 1] = total
                for c in s2_copies(u, i):
                    c.start()
        on_own(u, do)

    def stage3(u):
        n_ = lax.rem(u, SLOTS)

        def begin(which):
            for c in state_copies(u)[0][which]:
                c.start()
        on_matrix(u, begin)
        for i in range(KINDS):
            s2_copies(u, i)[0].wait()
            q1[n_, i] = (q1[n_, i].astype(F32) + t3[n_, i, 0]).astype(BF)
            s3_copy(u, i).start()

    def stage4(u):
        n_, z = lax.rem(u, SLOTS), lax.rem(u, 2)

        def update(g, w, m, v):
            g = g.astype(BF).astype(F32)
            m = 0.9 * m + 0.1 * g
            v = 0.95 * v + 0.05 * g * g
            w = w.astype(F32)
            return (w - 0.02 * (m * lax.rsqrt(v + 1e-8) + 0.1 * w)).astype(BF), m, v

        for i in range(KINDS):
            s2_copies(u, i)[1].wait()
            s3_copy(u, i).wait()

        def do(which):
            for c in state_copies(u)[0][which]:
                c.wait()
            wide, sub = d // KINDS, sub_g if which < 2 else sub_d
            for i in range(KINDS):
                for c in range(r1.shape[3] // sub):
                    part = pl.ds(c * sub, sub)
                    g = q2[n_, i, part, :].astype(F32) + q3[n_, i, part, :].astype(F32) + t3[n_, i, 1, part, :]
                    if which < 2:
                        at = (z, pl.ds(i * sub, sub), pl.ds(c * LANES, LANES))
                        nw[at], nm[at], nv[at] = update(g, cw[at], cm[at], cv[at])
                    else:
                        at = (z, slice(None), pl.ds(i * wide + c * LANES, LANES))
                        fw[at], fm[at], fv[at] = update(g, ew[at], em[at], ev[at])
                for c in s4_copies(u, i, which):
                    c.start()
            for c in state_copies(u)[1][which]:
                c.start()
        on_matrix(u, do)

    def stage5(u):
        def do(which):
            for c in state_copies(u)[1][which]:
                c.wait()
            for i in range(KINDS):
                for c in s4_copies(u, i, which):
                    c.wait()
                s5_copy(u, i, which).start()
        on_matrix(u, do)

    def stage6(u):
        def do(which):
            for i in range(KINDS):
                s5_copy(u, i, which).wait()
                for c in s6_copies(u, i, which):
                    c.start()
        on_matrix(u, do)

    def stage7(u):
        def do(which):
            for i in range(KINDS):
                for c in s6_copies(u, i, which):
                    c.wait()
                s7_copy(u, i, which).start()
        on_matrix(u, do)

    def stage8(u):
        def do(which):
            for i in range(KINDS):
                s7_copy(u, i, which).wait()
        on_matrix(u, do)

    stages = (stage0, stage1, stage2, stage3, stage4, stage5, stage6, stage7, stage8)

    def tick(t, _):
        for k, stage in enumerate(stages):
            u = t - 1 - k
            pl.when((u >= 0) & (u < units))(functools.partial(stage, u))

        layer, _, j, k = place(t)
        busy = t < units
        even = lax.rem(k, 2) == 0
        pl.when(busy & (k < 2 * BLOCKS) & even)(lambda: hidden_block(layer, j, lax.rem(t, ring)))
        pl.when(busy & (k < 2 * BLOCKS) & ~even)(
            lambda: hidden_rest(layer, j, lax.rem(t, ring), (layers - 1 - layer) * BLOCKS))
        pl.when(busy & (k >= 2 * BLOCKS) & (layer > 0))(lambda: states_back(layer, j))
        return 0

    lax.fori_loop(0, units + len(stages), tick, 0)


def train_step(layers, a0, a1, h1, dy, ws, ms, vs):
    n, d = dy.shape
    f = ws[0].shape[2] // BLOCKS
    owners = SIDE * SIDE
    rows_g, rows_d = d // owners, f * BLOCKS // owners
    units = layers * 3 * BLOCKS
    ring, dring = 4, 7
    flat = rows_g * f // KINDS // LANES
    blocks = (SLOTS, KINDS, SIDE, flat, LANES)
    block = (SLOTS, KINDS, flat, LANES)
    gate, down = (2, rows_g, f), (2, rows_d // BLOCKS, d)
    vmem, dma = pltpu.VMEM, pltpu.SemaphoreType.DMA
    sd = jax.ShapeDtypeStruct
    outs = pl.pallas_call(
        functools.partial(step_kernel, layers=layers, units=units, ring=ring, dring=dring),
        out_shape=[sd((layers, SIDE, SIDE, rows_g, d and f * BLOCKS), BF)] * 2
        + [sd((layers, SIDE, SIDE, rows_d, d), BF)]
        + [sd(m.shape, F32) for m in ms] + [sd(v.shape, F32) for v in vs]
        + [sd((n, f * BLOCKS), BF)] * 2,
        in_specs=[ANY] * 13,
        out_specs=[ANY] * 11,
        scratch_shapes=[
            vmem((n, d), BF), vmem((n, d), BF), vmem((d, f), BF), vmem((d, f), BF), vmem((f, d), BF),
            vmem((n, f), BF), vmem((n, f), BF), vmem((n, f), BF), vmem((n, d), F32),
            vmem((ring, KINDS, SIDE, SIDE, flat, LANES), BF), vmem((dring, KINDS, SIDE, SIDE, flat, LANES), BF),
            vmem(blocks, BF), vmem(blocks, BF), vmem(blocks, BF), vmem((SLOTS, KINDS, 2, flat, LANES), F32),
            vmem(block, BF), vmem(block, BF), vmem(block, BF),
            vmem(gate, BF), vmem(gate, F32), vmem(gate, F32), vmem(gate, BF), vmem(gate, F32), vmem(gate, F32),
            vmem(down, BF), vmem(down, F32), vmem(down, F32), vmem(down, BF), vmem(down, F32), vmem(down, F32),
            dma((SLOTS, KINDS, 12)), dma((SLOTS, KINDS, 12)),
            dma((3,)), dma((2,)), dma((2,)), dma((2,)), dma((2, 3)), dma((2, 3)),
        ],
        compiler_params=pltpu.CompilerParams(collective_id=0, has_side_effects=True, vmem_limit_bytes=67043328),
        name="train_step",
    )(a0, a1, h1, dy, *ws, *ms, *vs)
    return outs[:9]


def solution(mesh):
    assert mesh.shape["dp"] == SIDE * SIDE

    def body(x, dy, *arrays):
        ws, ms, vs = (arrays[i : i + 3] for i in (0, 3, 6))
        x, dy = x[0], dy[0]
        a0, h1, a1 = first_layer(x, *ws)
        outs = train_step(ws[0].shape[0], a0, a1, h1, dy, ws, ms, vs)
        return tuple(o.reshape(w.shape) for o, w in zip(outs[:3], ws, strict=True)) + tuple(outs[3:])

    whole, rows = P(None, None, None), P(None, "dp", None)
    return jax.shard_map(
        body,
        mesh=mesh,
        in_specs=(P(("rep", "dp")),) * 2 + (whole,) * 3 + (rows,) * 6,
        out_specs=(P("rep"),) * 3 + (P("rep", "dp"),) * 6,
        check_vma=False,
    )
```

time: 1050 us -> 598 us (0.57)
  Pallas kernels: 0 us -> 559 us
  waiting for transfers between devices: 550 us -> 0 us
  matrix products: 372 us -> 0 us
  other arithmetic: 60.8 us -> 0.01 us
  between operations: 14.6 us -> 0.69 us
    pallas_call x0 -> x2, Pallas kernels: none -> 559 us  [the longest x1 487 us: train_step(): pl.pallas_call(functools.partial(step_kernel, layers=layers, units=units,...]
    dot_general x15 -> x0, matrix products: 372 us -> none  [the longest x5 137 us: layer(): gate = jnp.dot(a, w['w_gate'], preferred_element_type=jnp.float32)]
    all_gather x6 -> x0, waiting for transfers between devices: 317 us -> none  [body(): new[k][n] = (lax.all_gather(w, 'dp', axis=0, tiled=True), mm, vv)]
    reduce_scatter x4 -> x0, waiting for transfers between devices: 230 us -> none  [body(): g = lax.psum_scatter(grads[NAMES[k]], 'dp', scatter_dimension=0, tiled=True)]
    another operation x6 -> x0, other arithmetic: 38.4 us -> none  [body(): jnp.stack([one[which] for one in new[k]])]
    slice x3 -> x0, local copies, waits for them, and re-layouts: 31.5 us -> none  [the longest x2 21.1 us: body(): w[n]]
    unnamed x30 -> x31, local copies, waits for them, and re-layouts: 15.9 us -> 38 us
    convert_element_type x3 -> x0, other arithmetic: 13.9 us -> none  [adamw(): return ((w - 0.02 * step).astype(jnp.bfloat16), m, v)]
  transfers between devices with their start and end apart: 12 -> 0, of which waited for: 10 -> 0; matrix products, arithmetic and copies ran while one was open for 26% -> 0% of each run, Pallas kernels for 0% -> 0%
where the time goes in v2:
time: 598 us; the launch traced here: 597 us
  Pallas kernels  559 us (93%)
  local copies, waits for them, and re-layouts  38 us (6%)
    pallas_call x1, Pallas kernels, train_step(): pl.pallas_call(functools.partial(step_kernel, layers=layers, units=units,...  487 us
    pallas_call x1, Pallas kernels, first_layer(): pl.pallas_call(functools.partial(forward_kernel, rows=256), grid=(BLOCKS,...  71.7 us
    unnamed x31, local copies, waits for them, and re-layouts  38 us

profile of v2, /device:TPU:96, one launch (start us, length us, event | category | flops | bytes accessed | tf_op | source)
XLA Modules:
  0.0 597.3 jit_solution(6771925703959074619)
XLA Ops:
  0.6 71.7 %first_layer.1 = (bf16[2048,1024]{1,0:T(8,128)(2,1)}, bf16[2048,1024]{1,0:T(8,128)(2,1)}, bf16[2048,1024]{1,0:T(8,128)(2,1)}) custom-call(bf16[2048,1024]{1,0:T(8,128)(2,1)} %bitcast.11, bf16[2,1024,3200]{2,1,0:T(8,128)(2,1)} %wg_h.1, bf16[2,1024,3200]{2,1,0:T(8,128)(2,1)} %wu_h.1, bf16[2,3200,1024]{2,1,0:T(8,128)(2,1)} %wd_h.1), custom_call_target="tpu_custom_call" | custom-call | tf_op jit(solution)/shard_map/first_layer/pallas_call | solution.py:68
  72.3 486.9 %train_step.1 = (bf16[2,4,4,64,3200]{4,3,2,1,0:T(8,128)(2,1)}, bf16[2,4,4,64,3200]{4,3,2,1,0:T(8,128)(2,1)}, bf16[2,4,4,200,1024]{4,3,2,1,0:T(8,128)(2,1)}, f32[...) custom-call(bf16[2048,1024]{1,0:T(8,128)(2,1)} %get-tuple-element.21, ...), custom_call_target="tpu_custom_call" | custom-call | tf_op jit(solution)/shard_map/train_step/pallas_call | solution.py:542
  559.2 0.0 copy-start
  559.2 0.0 slice-start
  559.2 0.0 slice-start.1
  559.2 12.7 %copy.29 = bf16[2,1024,3200]{2,1,0:T(8,128)(2,1)} copy(bf16[2,1024,3200]{2,1,0:T(8,128)(2,1)} %bitcast.9) | data formatting | bytes 26214400
  571.9 0.0 copy-done
  571.9 0.0 slice-start.2
  571.9 0.0 slice-start.3
  571.9 6.6 %copy.30 = bf16[2,1024,3200]{2,1,0:T(8,128)(2,1)} copy(bf16[2,1024,3200]{2,1,0:T(8,128)(2,1)S(1)} %bitcast.8) | data formatting | bytes 26214400
  578.6 0.0 slice-done
  578.6 1.2 slice-done.1
  579.7 1.3 slice-done.2
  581.0 0.0 slice-done.3
  581.0 0.0 copy-start.6
  581.0 4.9 copy.31
  586.0 0.0 copy-done.6
  586.0 0.0 copy-start.5
  586.0 1.2 copy.32
  587.1 0.9 copy-done.5
  588.0 0.0 copy-start.4
  588.0 1.2 copy.33
  589.2 0.9 copy-done.4
  590.0 0.0 copy-start.3
  590.0 1.2 copy.34
  591.2 0.9 copy-done.3
  592.0 0.0 copy-start.2
  592.1 1.2 copy.35
  593.2 0.9 copy-done.2
  594.1 0.0 copy-start.1
  594.1 1.2 copy.36
  595.2 0.9 copy-done.1
  596.1 1.2 copy.37
  (1 shorter events, 0.0 us)
Async XLA Ops:
  559.2 12.7 %copy-start = (bf16[2,4,4,64,3200]{4,3,2,1,0:T(8,128)(2,1)S(1)}, bf16[2,4,4,64,3200]{4,3,2,1,0:T(8,128)(2,1)}, u32[]{:S(2)}) copy-start(bf16[2,4,4,64,3200]{4,3,2,1,0:T(8,128)(2,1)} %get-tuple-element.25) | copy-start | bytes 39321604
  559.2 19.4 %slice-start = ((s8[13107200]{0:T(1024)(128)(4,1)}), s8[4194304]{0:T(1024)(128)(4,1)S(1)}, s32[]{:S(2)}) async-start(s8[13107200]{0:T(1024)(128)(4,1)} %bitcast.5), calls=%async_computation | async-start | bytes 8388608
  559.2 20.5 %slice-start.1 = ((s8[13107200]{0:T(1024)(128)(4,1)}), s8[4194304]{0:T(1024)(128)(4,1)S(1)}, s32[]{:S(2)}) async-start(s8[13107200]{0:T(1024)(128)(4,1)} %bitcast.5), calls=%async_computation.1 | async-start | bytes 8388608
  571.9 9.1 %slice-start.2 = ((s8[13107200]{0:T(1024)(128)(4,1)}), s8[4194304]{0:T(1024)(128)(4,1)S(1)}, s32[]{:S(2)}) async-start(s8[13107200]{0:T(1024)(128)(4,1)} %bitcast.5), calls=%async_computation.2 | async-start | bytes 8388608
  571.9 9.1 %slice-start.3 = ((s8[13107200]{0:T(1024)(128)(4,1)}), s8[524288]{0:T(1024)(128)(4,1)S(1)}, s32[]{:S(2)}) async-start(s8[13107200]{0:T(1024)(128)(4,1)} %bitcast.5), calls=%async_computation.3 | async-start | bytes 1048576
  581.0 5.0 copy-start.6
  586.0 2.0 copy-start.5
  588.0 2.0 copy-start.4
  590.0 2.0 copy-start.3
  592.0 2.0 copy-start.2
  594.1 2.0 copy-start.1

commit v3 on v1

v3 whole, which is shorter than its diff:
```python
import functools

import jax
import jax.numpy as jnp
from jax import lax
from jax.experimental import pallas as pl
from jax.experimental.pallas import tpu as pltpu
from jax.sharding import PartitionSpec as P

BF, F32 = jnp.bfloat16, jnp.float32
MESH = pl.DeviceIdType.MESH
SIDE = 4
KINDS = 4
BLOCKS = 5
LANES = 128
SPLIT = 1
WHEN = (0, 1, 2, 3, 4, 5, 7, 8, 9)
UNROLL = 4
VLIM = 38 * 2**20
SLOTS = 4
ANY = pl.BlockSpec(memory_space=pl.ANY)


def dot(a, b, da, db):
    return lax.dot_general(a, b, (((da,), (db,)), ((), ())), preferred_element_type=F32)


def normed(wide):
    return (wide * lax.rsqrt(jnp.mean(wide * wide, -1, keepdims=True) + 1e-6)).astype(BF)


def step_kernel(x_h, dy_h, wg_h, wu_h, wd_h, mg_h, mu_h, md_h, vg_h, vu_h, vd_h,
                og_h, ou_h, od_h, omg_h, omu_h, omd_h, ovg_h, ovu_h, ovd_h, both_h, a, h, dy, wgu, hid, both,
                wd, acc, dwg, dwd,
                r1, r2, r3, t3, q1, q2, q3,
                cw, cm, cv, nw, nm, nv, ew, em, ev, fw, fm, fv,
                ss, rs, lw, la, lb, ls, lp, lo, lf, *, layers, units, ring):
    n, d = a.shape
    f = wd.shape[1]
    rows_g = d // (SIDE * SIDE)
    rows_d = f * BLOCKS // (SIDE * SIDE)
    sub_g, sub_d = rows_g // KINDS, rows_d // BLOCKS
    per_layer = units // layers
    me = lax.axis_index("dp")
    mx, my = me // SIDE, me % SIDE
    wrap = lambda v: lax.rem(v + 2 * SIDE, SIDE)
    dev = lambda x, y: {"dp": wrap(x) * SIDE + wrap(y)}

    barrier = pltpu.get_barrier_semaphore()
    for x, y in ((mx + 1, my), (mx - 1, my), (mx, my + 1), (mx, my - 1)):
        pl.semaphore_signal(barrier, inc=1, device_id=dev(x, y), device_id_type=MESH)

    load = lambda src, dst, sem: lambda: pltpu.make_async_copy(src, dst, sem)

    def start(*copies):
        for c in copies:
            c().start()

    def wait(*copies):
        for c in copies:
            c().wait()

    def weights(w):
        z, b, turn = lax.rem(w, 2), lax.rem(w, BLOCKS), w // BLOCKS
        layer = jnp.where((turn == 0) | (turn == 3), 0, layers - 1)
        cols = pl.ds(pl.multiple_of(b * f, LANES), f)
        rows = pl.ds(pl.multiple_of(b * f, 8), f)
        return (load(wg_h.at[layer, :, cols], wgu.at[z, :, pl.ds(0, f)], lw.at[z, 0]),
                load(wu_h.at[layer, :, cols], wgu.at[z, :, pl.ds(f, f)], lw.at[z, 1]),
                load(wd_h.at[layer, rows, :], wd.at[z], lw.at[z, 2]))

    def next_weights(w):
        wait(*weights(w))
        pl.when(w < 4 * BLOCKS - 1)(lambda: start(*weights(w + 1)))

    saved = lambda b: load(both, both_h.at[b], ls)
    back = lambda b: load(both_h.at[b], both, lb.at[0])
    TILE, NORM = 256, 64
    load_x = [load(x_h.at[pl.ds(t * TILE, TILE), :], h.at[pl.ds(t * TILE, TILE), :], la.at[t]) for t in range(n // TILE)]
    load_dy = load(dy_h, dy, lb.at[1])
    start(load_x[0], *weights(0), *load_x[1:])

    def tokens(t, size=TILE):
        return pl.ds(pl.multiple_of(t * size, size), size)

    def loop(count, do, unroll):
        def some(t, _):
            for k in range(unroll):
                do(t * unroll + k)
            return 0

        lax.fori_loop(0, count // unroll, some, 0)

    def every_token(do, size=NORM, unroll=1):
        loop(n // size, lambda t: do(tokens(t, size)), unroll)

    def norm_states(at):
        a[at, :] = normed(h[at, :].astype(F32))

    def first_units(b):
        z = lax.rem(b, 2)
        at_start, at_end = isinstance(b, int) and b == 0, isinstance(b, int) and b == BLOCKS - 1
        next_weights(b)

        def do(t):
            at = tokens(t)
            if at_start:
                pltpu.make_async_copy(x_h.at[at, :], h.at[at, :], la.at[t]).wait()
                norm_states(at)
            gu = dot(a[at, :], wgu[z], 1, 0)
            gate, up = gu[:, :f], gu[:, f:]
            hidden = (gate * jax.nn.sigmoid(gate) * up).astype(BF)
            more = dot(hidden, wd[z], 1, 0)
            if at_end:
                new = h[at, :] + (acc[at, :] + more).astype(BF)
                h[at, :] = new
                a[at, :] = normed(new.astype(F32))
            else:
                acc[at, :] = more if at_start else acc[at, :] + more

        loop(n // TILE, do, UNROLL)

    def clear(at):
        acc[at, :] = jnp.zeros((NORM, d), F32)

    def hidden_units(layer, b, piece):
        w = jnp.where(layer > 0, BLOCKS, 3 * BLOCKS) + b
        z = lax.rem(w, 2)

        @pl.when(piece == 0)
        def _():
            next_weights(w)

            @pl.when((b == 0) & (layer == 0))
            def _():
                wait(*load_x)
                every_token(norm_states)

            @pl.when((b == 0) & (layer > 0))
            def _():
                wait(load_dy)

        def part(t):
            at = tokens(piece * (n // TILE // (2 * SPLIT)) + t)
            gu = dot(a[at, :], wgu[z], 1, 0)
            gate, up = gu[:, :f], gu[:, f:]
            back = dot(dy[at, :], wd[z], 1, 1).astype(BF).astype(F32)
            s = jax.nn.sigmoid(gate)
            silu = gate * s
            hid[at, :] = (silu * up).astype(BF)
            both[at, f:] = (back * silu).astype(BF)
            both[at, :f] = (back * up * (s + silu * (1 - s))).astype(BF)

        loop(n // TILE // (2 * SPLIT), part, UNROLL)
        pl.when((piece == 2 * SPLIT - 1) & (layer > 0))(lambda: start(saved(b)))

    def gradient_columns(u, piece):
        quarter = d // SIDE

        def part(r):
            r = piece * (SIDE // SPLIT) + r
            cols = pl.ds(pl.multiple_of(r * quarter, LANES), quarter)
            g = dot(a[:, cols], both[...], 0, 0).astype(BF)
            g = g.reshape(SIDE, KINDS, sub_g, 2 * f)
            for which in range(2):
                slot = lax.rem(u + which, ring)
                for i in range(KINDS):
                    for c in range(f // LANES):
                        at = which * f + c * LANES
                        dwg[slot, i, r, :, c * sub_g : (c + 1) * sub_g, :] = g[:, i, :, at : at + LANES]

        loop(SIDE // SPLIT, part, UNROLL)

    def gradient_rows(layer, b, piece):
        cols_k = d // KINDS

        def part(i):
            i = piece * (KINDS // SPLIT) + i
            cols = pl.ds(pl.multiple_of(i * cols_k, LANES), cols_k)
            g = dot(hid[...], dy[:, cols], 0, 0).astype(BF)
            for k in range(f // sub_d):
                unit = b * (f // sub_d) + k
                owner, j = unit // BLOCKS, unit % BLOCKS
                slot = lax.rem((layers - 1 - layer) * BLOCKS + j, dwd.shape[0])
                for c in range(cols_k // LANES):
                    dwd[slot, i, owner // SIDE, owner % SIDE, c * sub_d : (c + 1) * sub_d, :] = (
                        g[k * sub_d : (k + 1) * sub_d, c * LANES : (c + 1) * LANES])

        loop(KINDS // SPLIT, part, UNROLL)

        @pl.when((layer > 0) & (piece == SPLIT - 1))
        def _():
            wait(saved(b))
            pl.when(b == BLOCKS - 1)(lambda: start(back(0)))

    def states_back(q, piece):
        w = 2 * BLOCKS + q
        z = lax.rem(w, 2)

        @pl.when(piece == 0)
        def _():
            pl.when(q == 0)(lambda: every_token(clear))
            next_weights(w)
            wait(back(q))

        def part(t):
            at = tokens(piece * (n // TILE // (2 * SPLIT)) + t)
            acc[at, :] = acc[at, :] + dot(both[at, :], wgu[z], 1, 1)

        loop(n // TILE // (2 * SPLIT), part, UNROLL)
        pl.when((piece == 2 * SPLIT - 1) & (q < BLOCKS - 1))(lambda: start(back(q + 1)))

        @pl.when((piece == 2 * SPLIT - 1) & (q == BLOCKS - 1))
        def _():
            def do(at):
                wide = h[at, :].astype(F32)
                scale = lax.rsqrt(jnp.mean(wide * wide, -1, keepdims=True) + 1e-6)
                by = acc[at, :].astype(BF).astype(F32)
                along = jnp.mean(by * wide, -1, keepdims=True)
                more = by * scale - wide * (scale * scale * scale * along)
                dy[at, :] = (dy[at, :].astype(F32) + more.astype(BF).astype(F32)).astype(BF)

            every_token(do)
            start(*load_x)

    def place(u):
        k = lax.rem(u, per_layer)
        return layers - 1 - u // per_layer, jnp.where(k >= 2 * BLOCKS, k - 2 * BLOCKS, k // 2)

    def steps(i):
        s = 1 - 2 * (i % 2)
        xs, ys = (dev(mx + s, my), dev(mx - s, my)), (dev(mx, my + s), dev(mx, my - s))
        return (*xs, *ys, mx, my, s) if i < 2 else (*ys, *xs, my, mx, s)

    def rcopy(src, dst, u, i, k, to):
        n_ = lax.rem(u, SLOTS)
        return lambda: pltpu.make_async_remote_copy(
            src_ref=src, dst_ref=dst, send_sem=ss.at[n_, i, k], recv_sem=rs.at[n_, i, k], device_id=to, device_id_type=MESH)

    def own(u, i, p, which):
        w = dwd.at[lax.rem(u // per_layer * BLOCKS + place(u)[1], dwd.shape[0]), i] if which else dwg.at[lax.rem(u, ring), i]
        return w.at[p] if i < 2 else w.at[:, p]

    def on_own(u, do):
        k = lax.rem(u, per_layer)
        pl.when(k < 2 * BLOCKS)(lambda: do(0))
        pl.when(k >= 2 * BLOCKS)(lambda: do(1))

    def s0_copies(u, i, which):
        ahead, behind, _, _, pf, _, s = steps(i)
        n_ = lax.rem(u, SLOTS)
        return (rcopy(own(u, i, wrap(pf + 2), which), r1.at[n_, i], u, i, 0, ahead),
                rcopy(own(u, i, wrap(pf - s), which), r2.at[n_, i], u, i, 1, behind))

    def s1_copy(u, i):
        n_ = lax.rem(u, SLOTS)
        return rcopy(r1.at[n_, i], r3.at[n_, i], u, i, 2, steps(i)[0])

    def s2_copies(u, i):
        _, _, ahead, behind, _, ps, s = steps(i)
        n_ = lax.rem(u, SLOTS)
        return (rcopy(r3.at[n_, i, wrap(ps + 2)], q1.at[n_, i], u, i, 3, ahead),
                rcopy(r3.at[n_, i, wrap(ps - s)], q2.at[n_, i], u, i, 4, behind))

    def s3_copy(u, i):
        n_ = lax.rem(u, SLOTS)
        return rcopy(q1.at[n_, i], q3.at[n_, i], u, i, 5, steps(i)[2])

    def state_copies(u, which, out):
        layer, j = place(u)
        z = lax.rem(u, 2)
        cols = pl.ds(pl.multiple_of(j * f, LANES), f)
        rows = pl.ds(pl.multiple_of(me * rows_d + j * sub_d, 8), sub_d)
        mine = pl.ds(pl.multiple_of(j * sub_d, 8), sub_d)
        first = pl.ds(pl.multiple_of(me * rows_g, 8), rows_g)
        if which < 2:
            if out:
                w, m, v = ((og_h, omg_h, ovg_h), (ou_h, omu_h, ovu_h))[which]
                return (load(nw.at[z], w.at[layer, mx, my, :, cols], lo.at[z, 0]), load(nm.at[z], m.at[layer, :, cols], lo.at[z, 1]),
                        load(nv.at[z], v.at[layer, :, cols], lo.at[z, 2]))
            w, m, v = ((wg_h, mg_h, vg_h), (wu_h, mu_h, vu_h))[which]
            return (load(w.at[layer, first, cols], cw.at[z], lp.at[z, 0]), load(m.at[layer, :, cols], cm.at[z], lp.at[z, 1]),
                    load(v.at[layer, :, cols], cv.at[z], lp.at[z, 2]))
        if out:
            return (load(fw.at[z], od_h.at[layer, mx, my, mine, :], lo.at[z, 0]), load(fm.at[z], omd_h.at[layer, mine, :], lo.at[z, 1]),
                    load(fv.at[z], ovd_h.at[layer, mine, :], lo.at[z, 2]))
        return (load(wd_h.at[layer, rows, :], ew.at[z], lp.at[z, 0]), load(md_h.at[layer, mine, :], em.at[z], lp.at[z, 1]),
                load(vd_h.at[layer, mine, :], ev.at[z], lp.at[z, 2]))

    def on_matrix(u, do):
        k = lax.rem(u, per_layer)
        down = k >= 2 * BLOCKS
        for which, test in enumerate((~down & (lax.rem(k, 2) == 0), ~down & (lax.rem(k, 2) == 1), down)):
            pl.when(test)(functools.partial(do, which))

    def out_at(u, i, which):
        layer, j = place(u)
        if which < 2:
            cols = pl.ds(pl.multiple_of(j * f, LANES), f)
            return lambda x, y: (og_h, ou_h)[which].at[layer, x, y, pl.ds(i * sub_g, sub_g), cols]
        rows = pl.ds(pl.multiple_of(j * sub_d, 8), sub_d)
        wide = d // KINDS
        return lambda x, y: od_h.at[layer, x, y, rows, pl.ds(i * wide, wide)]

    def s4_copies(u, i, which):
        _, _, ahead, behind, _, _, _ = steps(i)
        z = lax.rem(u, 2)
        wide = d // KINDS
        dst = out_at(u, i, which)(mx, my)
        src = nw.at[z, pl.ds(i * sub_g, sub_g), :] if which < 2 else fw.at[z, :, pl.ds(i * wide, wide)]
        return (rcopy(src, dst, u, i, 6, ahead), rcopy(src, dst, u, i, 7, behind))

    def s5_copy(u, i, which):
        _, _, ahead, _, pf, ps, s = steps(i)
        at = out_at(u, i, which)
        src = at(pf, wrap(ps - s)) if i < 2 else at(wrap(ps - s), pf)
        return rcopy(src, src, u, i, 8, ahead)

    every = pl.ds(0, SIDE)

    def s6_copies(u, i, which):
        ahead, behind, _, _, pf, _, _ = steps(i)
        at = out_at(u, i, which)
        src = at(pf, every) if i < 2 else at(every, pf)
        return (rcopy(src, src, u, i, 9, ahead), rcopy(src, src, u, i, 10, behind))

    def s7_copy(u, i, which):
        ahead, _, _, _, pf, _, s = steps(i)
        at = out_at(u, i, which)
        p = wrap(pf - s)
        src = at(p, every) if i < 2 else at(every, p)
        return rcopy(src, src, u, i, 11, ahead)

    def stage0(u):
        def do(which):
            for i in range(KINDS):
                start(*s0_copies(u, i, which))
        on_own(u, do)

    def stage1(u):
        n_ = lax.rem(u, SLOTS)

        def do(which):
            for i in range(KINDS):
                _, _, _, _, pf, _, s = steps(i)
                wait(s0_copies(u, i, which)[0])
                mine = own(u, i, wrap(pf + s), which)
                r1[n_, i] = (r1[n_, i].astype(F32) + mine[...].astype(F32)).astype(BF)
                start(s1_copy(u, i))
        on_own(u, do)

    def stage2(u):
        n_ = lax.rem(u, SLOTS)

        def do(which):
            for i in range(KINDS):
                _, _, _, _, pf, ps, s = steps(i)
                wait(s0_copies(u, i, which)[1], s1_copy(u, i))
                mine = own(u, i, pf, which)
                for k in (2, -s, s, 0):
                    p = wrap(ps + k)
                    total = r2[n_, i, p].astype(F32) + r3[n_, i, p].astype(F32) + mine[p].astype(F32)
                    if k in (2, -s):
                        r3[n_, i, p] = total.astype(BF)
                    else:
                        t3[n_, i, 0 if k else 1] = total
                start(*s2_copies(u, i))
        on_own(u, do)

    def stage3(u):
        n_ = lax.rem(u, SLOTS)
        on_matrix(u, lambda which: start(*state_copies(u, which, False)))
        for i in range(KINDS):
            wait(s2_copies(u, i)[0])
            q1[n_, i] = (q1[n_, i].astype(F32) + t3[n_, i, 0]).astype(BF)
            start(s3_copy(u, i))

    def stage4(u):
        n_, z = lax.rem(u, SLOTS), lax.rem(u, 2)

        def update(g, w, m, v):
            g = g.astype(BF).astype(F32)
            m = 0.9 * m + 0.1 * g
            v = 0.95 * v + 0.05 * g * g
            w = w.astype(F32)
            return (w - 0.02 * (m * lax.rsqrt(v + 1e-8) + 0.1 * w)).astype(BF), m, v

        for i in range(KINDS):
            wait(s2_copies(u, i)[1], s3_copy(u, i))

        def do(which):
            wait(*state_copies(u, which, False))
            wide, sub = d // KINDS, sub_g if which < 2 else sub_d
            for i in range(KINDS):
                for c in range(r1.shape[3] // sub):
                    part = pl.ds(c * sub, sub)
                    g = q2[n_, i, part, :].astype(F32) + q3[n_, i, part, :].astype(F32) + t3[n_, i, 1, part, :]
                    if which < 2:
                        at = (z, pl.ds(i * sub, sub), pl.ds(c * LANES, LANES))
                        nw[at], nm[at], nv[at] = update(g, cw[at], cm[at], cv[at])
                    else:
                        at = (z, slice(None), pl.ds(i * wide + c * LANES, LANES))
                        fw[at], fm[at], fv[at] = update(g, ew[at], em[at], ev[at])
                start(*s4_copies(u, i, which))
            start(*state_copies(u, which, True))
        on_matrix(u, do)

    def stage5(u):
        def do(which):
            wait(*state_copies(u, which, True))
            for i in range(KINDS):
                wait(*s4_copies(u, i, which))
                start(s5_copy(u, i, which))
        on_matrix(u, do)

    def stage6(u):
        def do(which):
            for i in range(KINDS):
                wait(s5_copy(u, i, which))
                start(*s6_copies(u, i, which))
        on_matrix(u, do)

    def stage7(u):
        def do(which):
            for i in range(KINDS):
                wait(*s6_copies(u, i, which))
                start(s7_copy(u, i, which))
        on_matrix(u, do)

    def stage8(u):
        def do(which):
            for i in range(KINDS):
                wait(s7_copy(u, i, which))
        on_matrix(u, do)

    stages = (stage0, stage1, stage2, stage3, stage4, stage5, stage6, stage7, stage8)
    parts, first = 2 * SPLIT, 3 * SPLIT

    last = layers - 1
    in_a = n // rows_d

    def keep():
        def some(o, _):
            x, y = o // SIDE, lax.rem(o, SIDE)
            to = pl.ds(pl.multiple_of(o * rows_g, 8), rows_g)
            for k, (w, wide) in enumerate(((og_h, wgu), (ou_h, both))):
                half = pl.ds(pl.multiple_of(k * d + o * rows_g, 8), rows_g)
                for c in range(2):
                    at = wide.at[c, to] if k == 0 else wide.at[pl.ds(pl.multiple_of(c * d + o * rows_g, 8), rows_g)]
                    start(load(w.at[last, x, y, :, pl.ds(c * 2 * f, 2 * f)], at, lf.at[2 * k + c]))
                start(load(w.at[last, x, y, :, pl.ds(4 * f, f)], hid.at[half], lf.at[4 + k]))
                start(load(w.at[0, x, y, :, pl.ds(0, d)], dy.at[half], lf.at[6 + k]))

            @pl.when(o < in_a)
            def _():
                start(load(od_h.at[last, x, y], a.at[pl.ds(pl.multiple_of(o * rows_d, 8), rows_d)], lf.at[8]))

            @pl.when(o >= in_a)
            def _():
                start(load(od_h.at[last, x, y], h.at[pl.ds(pl.multiple_of((o - in_a) * rows_d, 8), rows_d)], lf.at[9]))
            return 0

        lax.fori_loop(0, SIDE * SIDE, some, 0)

    def kept():
        half = pl.ds(0, d)
        for c in range(2):
            wait(load(both_h.at[0, half], wgu.at[c], lf.at[c]), load(both_h.at[0, half], both.at[pl.ds(c * d, d)], lf.at[2 + c]))
        for k in range(2):
            wait(load(both_h.at[0, half, pl.ds(0, f)], hid.at[pl.ds(k * d, d)], lf.at[4 + k]),
                 load(dy_h.at[half], dy.at[pl.ds(k * d, d)], lf.at[6 + k]))
        for k, (blocks, to) in enumerate(((in_a, a), (SIDE * SIDE - in_a, h))):
            rows = pl.ds(0, blocks * rows_d)
            wait(load(dy_h.at[rows], to.at[rows], lf.at[8 + k]))

    keep_at = max(first + parts * (per_layer + 3) + WHEN[-1] + 1, parts * (per_layer + 2 * BLOCKS))
    assert d <= 2 * f

    def tick(t, _):
        for when, stage in zip(WHEN, stages, strict=True):
            since = t - first - when + parts * WHEN[-1]
            u = since // parts - WHEN[-1]
            pl.when((u >= 0) & (u < units) & (lax.rem(since, parts) == 0))(functools.partial(stage, u))
        pl.when(t == keep_at)(keep)

        layer = layers - 1 - t // (parts * per_layer)
        k = lax.rem(t, parts * per_layer)
        b, piece, c = k // (2 * parts), lax.rem(k, 2 * parts), k - 2 * parts * BLOCKS
        busy, blocks, start_u = t < parts * units, k < 2 * parts * BLOCKS, (layers - 1 - layer) * per_layer + 2 * b
        pl.when(busy & blocks & (piece < 2 * SPLIT))(lambda: hidden_units(layer, b, piece))
        pl.when(busy & blocks & (piece // SPLIT == 2))(lambda: gradient_columns(start_u, piece - 2 * SPLIT))
        pl.when(busy & blocks & (piece // SPLIT == 3))(lambda: gradient_rows(layer, b, piece - 3 * SPLIT))
        pl.when(busy & ~blocks & (layer > 0))(lambda: states_back(c // parts, lax.rem(c, parts)))
        return 0

    first_units(0)
    start(load_dy)
    lax.fori_loop(1, BLOCKS - 1, lambda b, _: (first_units(b), 0)[1], 0)
    first_units(BLOCKS - 1)
    pl.semaphore_wait(barrier, 4)
    lax.fori_loop(0, first + parts * (units - 1) + WHEN[-1] + 1, tick, 0)
    kept()


def results_kernel(*refs, hidden, count):
    (og, ou, od), moments, kept = refs[:3], refs[3:9], refs[9:15]
    (rg, ru, rd), moved = refs[15:18], refs[18:24]
    bg, bu, bd, bufs, sems = refs[24], refs[25], refs[26], refs[27:33], refs[33]
    a, h, dy, wgu, hid, both = kept
    n, d = a.shape
    f, last = hid.shape[1], rg.shape[0] - 1
    copies = []

    def copy(src, dst):
        copies.append(pltpu.make_async_copy(src, dst, sems.at[len(copies)]))
        return copies[-1]

    through = []
    step = d // 4
    for w, buf, out in ((og, bg, rg), (ou, bu, ru)):
        for r in range(0, d, step):
            at = (pl.ds(r, step), pl.ds(d, hidden - d))
            through.append((copy(w.at[0, *at], buf.at[pl.ds(r, step)]), copy(buf.at[pl.ds(r, step)], out.at[0, *at])))
    step = hidden // 4
    for r in range(0, hidden, step):
        at = pl.ds(r, step)
        through.append((copy(od.at[0, at], bd.at[at]), copy(bd.at[at], rd.at[0, at])))
    for src, buf, out in zip(moments, bufs, moved, strict=True):
        for layer in range(last + 1):
            through.append((copy(src.at[layer], buf.at[layer]), copy(buf.at[layer], out.at[layer])))
    block = hidden // (SIDE * SIDE)
    rows = n // block * block
    straight = [copy(a.at[pl.ds(0, rows)], rd.at[last, pl.ds(0, rows)]), copy(h.at[pl.ds(0, hidden - rows)], rd.at[last, pl.ds(rows, hidden - rows)])]
    for k, out in enumerate((rg, ru)):
        for c in range(2):
            src = both.at[pl.ds(c * d, d)] if k else wgu.at[c]
            straight.append(copy(src, out.at[last, :, pl.ds(c * 2 * f, 2 * f)]))
        straight.append(copy(hid.at[pl.ds(k * d, d)], out.at[last, :, pl.ds(4 * f, f)]))
        straight.append(copy(dy.at[pl.ds(k * d, d)], out.at[0, :, pl.ds(0, d)]))
    assert len(copies) == count
    for i, _ in through:
        i.start()
    for c in straight:
        c.start()
    for i, o in through:
        i.wait()
        o.start()
    for c in (*straight, *(o for _, o in through)):
        c.wait()


def results(arrays, kept):
    (layers, d, hidden), moments = arrays[0].shape, arrays[3:]
    count = 2 * (4 + 4 + 4 + len(moments) * layers) + 10
    vmem = [pltpu.VMEM(s, t) for s, t in (((d, hidden - d), BF), ((d, hidden - d), BF), ((hidden, d), BF), *((m.shape, F32) for m in moments))]
    return pl.pallas_call(
        functools.partial(results_kernel, hidden=hidden, count=count),
        out_shape=[jax.ShapeDtypeStruct(a.shape, a.dtype) for a in arrays],
        in_specs=[pl.BlockSpec(memory_space=pltpu.HBM)] * len(arrays) + [pl.BlockSpec(memory_space=pltpu.VMEM)] * len(kept),
        out_specs=[pl.BlockSpec(memory_space=pltpu.HBM)] * len(arrays),
        scratch_shapes=vmem + [pltpu.SemaphoreType.DMA((count,))],
        compiler_params=pltpu.CompilerParams(vmem_limit_bytes=VLIM),
        name="results",
    )(*(pltpu.with_memory_space_constraint(a, pltpu.HBM) for a in arrays), *(pltpu.with_memory_space_constraint(a, pltpu.VMEM) for a in kept))


def train_step(layers, x, dy, ws, ms, vs):
    n, d = dy.shape
    f = ws[0].shape[2] // BLOCKS
    owners = SIDE * SIDE
    rows_g, rows_d = d // owners, f * BLOCKS // owners
    units = layers * 3 * BLOCKS
    ring = 4
    flat = rows_g * f // KINDS // LANES
    blocks = (SLOTS, KINDS, SIDE, flat, LANES)
    block = (SLOTS, KINDS, flat, LANES)
    gate, down = (2, rows_g, f), (2, rows_d // BLOCKS, d)
    vmem, dma = pltpu.VMEM, pltpu.SemaphoreType.DMA
    sd = jax.ShapeDtypeStruct
    outs = pl.pallas_call(
        functools.partial(step_kernel, layers=layers, units=units, ring=ring),
        out_shape=[sd((layers, SIDE, SIDE, rows_g, f * BLOCKS), BF)] * 2
        + [sd((layers, SIDE, SIDE, rows_d, d), BF)]
        + [sd(m.shape, F32) for m in ms] + [sd(v.shape, F32) for v in vs]
        + [sd((BLOCKS, n, 2 * f), BF)]
        + [vmem((n, d), BF)] * 3 + [vmem((2, d, 2 * f), BF), vmem((n, f), BF), vmem((n, 2 * f), BF)],
        in_specs=[ANY] * 11,
        out_specs=[ANY] * 10 + [pl.BlockSpec(memory_space=pltpu.VMEM)] * 6,
        scratch_shapes=[
            vmem((2, f, d), BF), vmem((n, d), F32),
            vmem((ring, KINDS, SIDE, SIDE, flat, LANES), BF), vmem((BLOCKS + 1, KINDS, SIDE, SIDE, flat, LANES), BF),
            vmem(blocks, BF), vmem(blocks, BF), vmem(blocks, BF), vmem((SLOTS, KINDS, 2, flat, LANES), F32),
            vmem(block, BF), vmem(block, BF), vmem(block, BF),
            vmem(gate, BF), vmem(gate, F32), vmem(gate, F32), vmem(gate, BF), vmem(gate, F32), vmem(gate, F32),
            vmem(down, BF), vmem(down, F32), vmem(down, F32), vmem(down, BF), vmem(down, F32), vmem(down, F32),
            dma((SLOTS, KINDS, 12)), dma((SLOTS, KINDS, 12)),
            dma((2, 3)), dma((n // 256,)), dma((2,)), dma, dma((2, 3)), dma((2, 3)), dma((10,)),
        ],
        compiler_params=pltpu.CompilerParams(collective_id=0, has_side_effects=True, vmem_limit_bytes=VLIM),
        name="train_step",
    )(x, dy, *ws, *ms, *vs)
    return outs[:9], outs[10:]


def solution(mesh):
    assert mesh.shape["dp"] == SIDE * SIDE

    def body(x, dy, *arrays):
        ws, ms, vs = (arrays[i : i + 3] for i in (0, 3, 6))
        x, dy = x[0], dy[0]
        layers = ws[0].shape[0]
        outs, kept = train_step(layers, x, dy, ws, ms, vs)
        return tuple(results([o.reshape(w.shape) for o, w in zip(outs[:3], ws, strict=True)] + list(outs[3:]), kept))

    whole, rows = P(None, None, None), P(None, "dp", None)
    return jax.shard_map(
        body,
        mesh=mesh,
        in_specs=(P(("rep", "dp")),) * 2 + (whole,) * 3 + (rows,) * 6,
        out_specs=(P("rep"),) * 3 + (P("rep", "dp"),) * 6,
        check_vma=False,
    )
```

time: 1050 us -> 548 us (0.52)
  waiting for transfers between devices: 550 us -> 0 us
  Pallas kernels: 0 us -> 547 us
  matrix products: 372 us -> 0 us
  other arithmetic: 60.8 us -> 0 us
  local copies, waits for them, and re-layouts: 47.4 us -> 0 us
  between operations: 14.6 us -> 0.81 us
    pallas_call x0 -> x2, Pallas kernels: none -> 547 us  [the longest x1 522 us: train_step(): pl.pallas_call(functools.partial(step_kernel, layers=layers, units=units,...]
    dot_general x15 -> x0, matrix products: 372 us -> none  [the longest x5 137 us: layer(): gate = jnp.dot(a, w['w_gate'], preferred_element_type=jnp.float32)]
    all_gather x6 -> x0, waiting for transfers between devices: 317 us -> none  [body(): new[k][n] = (lax.all_gather(w, 'dp', axis=0, tiled=True), mm, vv)]
    reduce_scatter x4 -> x0, waiting for transfers between devices: 230 us -> none  [body(): g = lax.psum_scatter(grads[NAMES[k]], 'dp', scatter_dimension=0, tiled=True)]
    another operation x6 -> x0, other arithmetic: 38.4 us -> none  [body(): jnp.stack([one[which] for one in new[k]])]
    slice x3 -> x0, local copies, waits for them, and re-layouts: 31.5 us -> none  [the longest x2 21.1 us: body(): w[n]]
    unnamed x30 -> x0, local copies, waits for them, and re-layouts: 15.9 us -> none
    convert_element_type x3 -> x0, other arithmetic: 13.9 us -> none  [adamw(): return ((w - 0.02 * step).astype(jnp.bfloat16), m, v)]
  transfers between devices with their start and end apart: 12 -> 0, of which waited for: 10 -> 0; matrix products, arithmetic and copies ran while one was open for 26% -> 0% of each run, Pallas kernels for 0% -> 0%
where the time goes in v3:
time: 548 us
  Pallas kernels  547 us (100%)
    pallas_call x1, Pallas kernels, train_step(): pl.pallas_call(functools.partial(step_kernel, layers=layers, units=units,...  522 us
    pallas_call x1, Pallas kernels, results(): pl.pallas_call(functools.partial(results_kernel, hidden=hidden, count=cou...  25.1 us

profile of v3, /device:TPU:96, one launch (start us, length us, event | category | flops | bytes accessed | tf_op | source)
XLA Modules:
  0.0 547.6 jit_solution(7070494761134183280)
XLA Ops:
  0.6 521.6 %train_step.1 = (bf16[2,4,4,64,3200]{4,3,2,1,0:T(8,128)(2,1)}, bf16[2,4,4,64,3200]{4,3,2,1,0:T(8,128)(2,1)}, bf16[2,4,4,200,1024]{4,3,2,1,0:T(8,128)(2,1)}, f32[...) custom-call(bf16[2048,1024]{1,0:T(8,128)(2,1)} %bitcast.8, ...), custom_call_target="tpu_custom_call" | custom-call | tf_op jit(solution)/shard_map/train_step/pallas_call | solution.py:580
  522.3 25.1 %results.1 = (bf16[2,1024,3200]{2,1,0:T(8,128)(2,1)}, bf16[2,1024,3200]{2,1,0:T(8,128)(2,1)}, bf16[2,3200,1024]{2,1,0:T(8,128)(2,1)}, f32[2,64,3200]{2,1,0:T(8,1...) custom-call(bf16[2,1024,3200]{2,1,0:T(8,128)(2,1)} %bitcast.5, ...), custom_call_target="tpu_custom_call" | custom-call | tf_op jit(solution)/shard_map/results/pallas_call | solution.py:556

commit v4 on v3

--- a/solution.py
+++ b/solution.py
@@ -13,7 +13,6 @@
 KINDS = 4
 BLOCKS = 5
 LANES = 128
-SPLIT = 1
 WHEN = (0, 1, 2, 3, 4, 5, 7, 8, 9)
 UNROLL = 4
 VLIM = 38 * 2**20
@@ -78,6 +77,7 @@
     TILE, NORM = 256, 64
     load_x = [load(x_h.at[pl.ds(t * TILE, TILE), :], h.at[pl.ds(t * TILE, TILE), :], la.at[t]) for t in range(n // TILE)]
     load_dy = load(dy_h, dy, lb.at[1])
+    x_to_a = load(x_h, a, lb.at[1])
     start(load_x[0], *weights(0), *load_x[1:])
 
     def tokens(t, size=TILE):
@@ -91,8 +91,8 @@
 
         lax.fori_loop(0, count // unroll, some, 0)
 
-    def every_token(do, size=NORM, unroll=1):
-        loop(n // size, lambda t: do(tokens(t, size)), unroll)
+    def every_token(do):
+        loop(n // NORM, lambda t: do(tokens(t, NORM)), 1)
 
     def norm_states(at):
         a[at, :] = normed(h[at, :].astype(F32))
@@ -131,17 +131,12 @@
         def _():
             next_weights(w)
 
-            @pl.when((b == 0) & (layer == 0))
-            def _():
-                wait(*load_x)
-                every_token(norm_states)
-
             @pl.when((b == 0) & (layer > 0))
             def _():
                 wait(load_dy)
 
         def part(t):
-            at = tokens(piece * (n // TILE // (2 * SPLIT)) + t)
+            at = tokens(piece * (n // TILE // 2) + t)
             gu = dot(a[at, :], wgu[z], 1, 0)
             gate, up = gu[:, :f], gu[:, f:]
             back = dot(dy[at, :], wd[z], 1, 1).astype(BF).astype(F32)
@@ -151,14 +146,14 @@
             both[at, f:] = (back * silu).astype(BF)
             both[at, :f] = (back * up * (s + silu * (1 - s))).astype(BF)
 
-        loop(n // TILE // (2 * SPLIT), part, UNROLL)
-        pl.when((piece == 2 * SPLIT - 1) & (layer > 0))(lambda: start(saved(b)))
-
-    def gradient_columns(u, piece):
+        loop(n // TILE // 2, part, UNROLL)
+        pl.when((piece == 1) & (layer > 0))(lambda: start(saved(b)))
+
+    def gradient_columns(u, low, high):
         quarter = d // SIDE
 
         def part(r):
-            r = piece * (SIDE // SPLIT) + r
+            r = low + r
             cols = pl.ds(pl.multiple_of(r * quarter, LANES), quarter)
             g = dot(a[:, cols], both[...], 0, 0).astype(BF)
             g = g.reshape(SIDE, KINDS, sub_g, 2 * f)
@@ -169,13 +164,12 @@
                         at = which * f + c * LANES
                         dwg[slot, i, r, :, c * sub_g : (c + 1) * sub_g, :] = g[:, i, :, at : at + LANES]
 
-        loop(SIDE // SPLIT, part, UNROLL)
-
-    def gradient_rows(layer, b, piece):
+        loop(high - low, part, high - low)
+
+    def gradient_rows(layer, b):
         cols_k = d // KINDS
 
         def part(i):
-            i = piece * (KINDS // SPLIT) + i
             cols = pl.ds(pl.multiple_of(i * cols_k, LANES), cols_k)
             g = dot(hid[...], dy[:, cols], 0, 0).astype(BF)
             for k in range(f // sub_d):
@@ -186,12 +180,12 @@
                     dwd[slot, i, owner // SIDE, owner % SIDE, c * sub_d : (c + 1) * sub_d, :] = (
                         g[k * sub_d : (k + 1) * sub_d, c * LANES : (c + 1) * LANES])
 
-        loop(KINDS // SPLIT, part, UNROLL)
-
-        @pl.when((layer > 0) & (piece == SPLIT - 1))
+        loop(KINDS, part, UNROLL)
+
+        @pl.when(layer > 0)
         def _():
             wait(saved(b))
-            pl.when(b == BLOCKS - 1)(lambda: start(back(0)))
+            pl.when(b == BLOCKS - 1)(lambda: start(back(0), x_to_a))
 
     def states_back(q, piece):
         w = 2 * BLOCKS + q
@@ -204,15 +198,27 @@
             wait(back(q))
 
         def part(t):
-            at = tokens(piece * (n // TILE // (2 * SPLIT)) + t)
+            at = tokens(piece * (n // TILE // 2) + t)
             acc[at, :] = acc[at, :] + dot(both[at, :], wgu[z], 1, 1)
 
-        loop(n // TILE // (2 * SPLIT), part, UNROLL)
-        pl.when((piece == 2 * SPLIT - 1) & (q < BLOCKS - 1))(lambda: start(back(q + 1)))
-
-        @pl.when((piece == 2 * SPLIT - 1) & (q == BLOCKS - 1))
+        loop(n // TILE // 2, part, UNROLL)
+        pl.when((piece == 1) & (q < BLOCKS - 1))(lambda: start(back(q + 1)))
+        half = n // NORM // 2
+
+        @pl.when((q == 1) | (q == 2))
         def _():
-            def do(at):
+            pl.when((q == 1) & (piece == 0))(lambda: wait(x_to_a))
+
+            def do(t):
+                at = tokens((2 * (q - 1) + piece) * (half // 2) + t, NORM)
+                a[at, :] = normed(a[at, :].astype(F32))
+
+            loop(half // 2, do, 1)
+
+        @pl.when(q == BLOCKS - 1)
+        def _():
+            def do(t):
+                at = tokens(piece * half + t, NORM)
                 wide = h[at, :].astype(F32)
                 scale = lax.rsqrt(jnp.mean(wide * wide, -1, keepdims=True) + 1e-6)
                 by = acc[at, :].astype(BF).astype(F32)
@@ -220,8 +226,7 @@
                 more = by * scale - wide * (scale * scale * scale * along)
                 dy[at, :] = (dy[at, :].astype(F32) + more.astype(BF).astype(F32)).astype(BF)
 
-            every_token(do)
-            start(*load_x)
+            loop(half, do, 1)
 
     def place(u):
         k = lax.rem(u, per_layer)
@@ -434,7 +439,7 @@
         on_matrix(u, do)
 
     stages = (stage0, stage1, stage2, stage3, stage4, stage5, stage6, stage7, stage8)
-    parts, first = 2 * SPLIT, 3 * SPLIT
+    parts, first = 2, 4
 
     last = layers - 1
     in_a = n // rows_d
@@ -485,12 +490,17 @@
 
         layer = layers - 1 - t // (parts * per_layer)
         k = lax.rem(t, parts * per_layer)
-        b, piece, c = k // (2 * parts), lax.rem(k, 2 * parts), k - 2 * parts * BLOCKS
-        busy, blocks, start_u = t < parts * units, k < 2 * parts * BLOCKS, (layers - 1 - layer) * per_layer + 2 * b
-        pl.when(busy & blocks & (piece < 2 * SPLIT))(lambda: hidden_units(layer, b, piece))
-        pl.when(busy & blocks & (piece // SPLIT == 2))(lambda: gradient_columns(start_u, piece - 2 * SPLIT))
-        pl.when(busy & blocks & (piece // SPLIT == 3))(lambda: gradient_rows(layer, b, piece - 3 * SPLIT))
-        pl.when(busy & ~blocks & (layer > 0))(lambda: states_back(c // parts, lax.rem(c, parts)))
+        b, piece, c = k // 4, lax.rem(k, 4), k - 4 * BLOCKS
+        busy, blocks, u = t < parts * units, k < 4 * BLOCKS, (layers - 1 - layer) * per_layer + 2 * b
+        pl.when(busy & blocks & (piece < 2))(lambda: hidden_units(layer, b, piece))
+        pl.when(busy & blocks & (piece == 2))(lambda: gradient_columns(u, 0, SIDE - 1))
+
+        @pl.when(busy & blocks & (piece == 3))
+        def _():
+            gradient_columns(u, SIDE - 1, SIDE)
+            gradient_rows(layer, b)
+
+        pl.when(busy & ~blocks & (layer > 0))(lambda: states_back(c // 2, lax.rem(c, 2)))
         return 0
 
     first_units(0)

time: 548 us -> 535 us (0.976)
  Pallas kernels: 547 us -> 534 us
    pallas_call x1, Pallas kernels: 522 us -> 509 us  [train_step(): pl.pallas_call(functools.partial(step_kernel, layers=layers, units=units,...]
where the time goes in v4:
time: 535 us
  Pallas kernels  534 us (100%)
    pallas_call x1, Pallas kernels, train_step(): pl.pallas_call(functools.partial(step_kernel, layers=layers, units=units,...  509 us
    pallas_call x1, Pallas kernels, results(): pl.pallas_call(functools.partial(results_kernel, hidden=hidden, count=cou...  25.1 us

profile of v4, /device:TPU:96, one launch (start us, length us, event | category | flops | bytes accessed | tf_op | source)
XLA Modules:
  0.0 534.7 jit_solution(16125068582604093623)
XLA Ops:
  0.6 508.7 %train_step.1 = (bf16[2,4,4,64,3200]{4,3,2,1,0:T(8,128)(2,1)}, bf16[2,4,4,64,3200]{4,3,2,1,0:T(8,128)(2,1)}, bf16[2,4,4,200,1024]{4,3,2,1,0:T(8,128)(2,1)}, f32[...) custom-call(bf16[2048,1024]{1,0:T(8,128)(2,1)} %bitcast.8, ...), custom_call_target="tpu_custom_call" | custom-call | tf_op jit(solution)/shard_map/train_step/pallas_call | solution.py:590
  509.4 25.1 %results.1 = (bf16[2,1024,3200]{2,1,0:T(8,128)(2,1)}, bf16[2,1024,3200]{2,1,0:T(8,128)(2,1)}, bf16[2,3200,1024]{2,1,0:T(8,128)(2,1)}, f32[2,64,3200]{2,1,0:T(8,1...) custom-call(bf16[2,1024,3200]{2,1,0:T(8,128)(2,1)} %bitcast.5, ...), custom_call_target="tpu_custom_call" | custom-call | tf_op jit(solution)/shard_map/results/pallas_call | solution.py:566

commit v5 on v4

--- a/solution.py
+++ b/solution.py
@@ -14,7 +14,7 @@
 BLOCKS = 5
 LANES = 128
 WHEN = (0, 1, 2, 3, 4, 5, 7, 8, 9)
-UNROLL = 4
+UNROLL = 2
 VLIM = 38 * 2**20
 SLOTS = 4
 ANY = pl.BlockSpec(memory_space=pl.ANY)
@@ -74,7 +74,7 @@
 
     saved = lambda b: load(both, both_h.at[b], ls)
     back = lambda b: load(both_h.at[b], both, lb.at[0])
-    TILE, NORM = 256, 64
+    TILE, NORM = 512, 64
     load_x = [load(x_h.at[pl.ds(t * TILE, TILE), :], h.at[pl.ds(t * TILE, TILE), :], la.at[t]) for t in range(n // TILE)]
     load_dy = load(dy_h, dy, lb.at[1])
     x_to_a = load(x_h, a, lb.at[1])
@@ -89,7 +89,10 @@
                 do(t * unroll + k)
             return 0
 
-        lax.fori_loop(0, count // unroll, some, 0)
+        if count == unroll:
+            some(0, 0)
+        else:
+            lax.fori_loop(0, count // unroll, some, 0)
 
     def every_token(do):
         loop(n // NORM, lambda t: do(tokens(t, NORM)), 1)
@@ -180,7 +183,7 @@
                     dwd[slot, i, owner // SIDE, owner % SIDE, c * sub_d : (c + 1) * sub_d, :] = (
                         g[k * sub_d : (k + 1) * sub_d, c * LANES : (c + 1) * LANES])
 
-        loop(KINDS, part, UNROLL)
+        loop(KINDS, part, KINDS)
 
         @pl.when(layer > 0)
         def _():

time: 535 us -> 532 us (level)
  no operation moved by 1% of the time
where the time goes in v5:
time: 532 us
  Pallas kernels  532 us (100%)
    pallas_call x1, Pallas kernels, train_step(): pl.pallas_call(functools.partial(step_kernel, layers=layers, units=units,...  506 us
    pallas_call x1, Pallas kernels, results(): pl.pallas_call(functools.partial(results_kernel, hidden=hidden, count=cou...  25.1 us

profile of v5, /device:TPU:96, one launch (start us, length us, event | category | flops | bytes accessed | tf_op | source)
XLA Modules:
  0.0 532.3 jit_solution(7856555896121229320)
XLA Ops:
  0.6 506.4 %train_step.1 = (bf16[2,4,4,64,3200]{4,3,2,1,0:T(8,128)(2,1)}, bf16[2,4,4,64,3200]{4,3,2,1,0:T(8,128)(2,1)}, bf16[2,4,4,200,1024]{4,3,2,1,0:T(8,128)(2,1)}, f32[...) custom-call(bf16[2048,1024]{1,0:T(8,128)(2,1)} %bitcast.8, ...), custom_call_target="tpu_custom_call" | custom-call | tf_op jit(solution)/shard_map/train_step/pallas_call | solution.py:593
  507.0 25.1 %results.1 = (bf16[2,1024,3200]{2,1,0:T(8,128)(2,1)}, bf16[2,1024,3200]{2,1,0:T(8,128)(2,1)}, bf16[2,3200,1024]{2,1,0:T(8,128)(2,1)}, f32[2,64,3200]{2,1,0:T(8,1...) custom-call(bf16[2,1024,3200]{2,1,0:T(8,128)(2,1)} %bitcast.5, ...), custom_call_target="tpu_custom_call" | custom-call | tf_op jit(solution)/shard_map/results/pallas_call | solution.py:569
